TPU v7x, 32 devices: a whole 2x2x4 slice. The times are simulated.
32 devices in a mesh: batch: 8 (over y, x, core), width: 4 (over z).
Axes of the slice: x: 2, y: 2, z: 4, core: 2. Of those that a mesh axis runs over, the one named last changes fastest.
Arguments:
- samples: bfloat16 [2048, 8192], P('batch', 'width'), parts along dimension 0, may hold values from -6 to 6
- rank_down: bfloat16 [8192, 2, 1024], P('width'), may hold values from -0.09375 to 0.09375
- rank_up: bfloat16 [1024, 2, 8192], P(None, None, 'width'), may hold values from -0.1875 to 0.1875
- gate_proj: bfloat16 [8192, 2], P('width'), may hold values from -0.0625 to 0.0625
- expert_bias: float32 [2, 8192], P(None, 'width'), may hold values from -3 to 3
Outputs:
- crossed: bfloat16 [2048, 8192], P('batch', 'width'), parts along dimension 0
There are 8 independent parts, one for each index of `batch`. A program takes and returns all parts, laid end to end along the dimension named above; an argument that names none is the same for every part. Nothing has to cross between parts.
All inputs are finite; a program needn't handle non-finite values.
Results may differ from a plain program's by a relative error of at most 0.0027.
Values may be sent and summed in bfloat16 or wider, within the bound.
No kernel may reach another device: no remote copies, remote signals or barrier semaphores. Data moves between devices by JAX's collectives and lax.ppermute only.
A program may use at most 64 MiB of HBM per device.

v0:
```python
import jax
import jax.numpy as jnp
from jax import lax
from jax.sharding import PartitionSpec as P


def shards(samples, rank_down, rank_up, gate_proj, expert_bias):
    logits = lax.psum(jnp.dot(samples, gate_proj, preferred_element_type=jnp.float32), "width")
    gating = jax.nn.sigmoid(logits)
    shares = lax.psum_scatter(
        jnp.einsum("fek,bf->keb", rank_down, samples, preferred_element_type=jnp.float32),
        "width",
        scatter_dimension=0,
        tiled=True,
    )
    hidden_share = jnp.tanh(shares).astype(jnp.bfloat16)
    expanded = jnp.einsum(
        "keb,kef->ebf",
        lax.all_gather(hidden_share, "width", axis=0, tiled=True),
        rank_up,
        preferred_element_type=jnp.float32,
    )
    blended = jnp.sum(
        jnp.transpose(gating)[:, :, None] * (expanded + expert_bias[:, None, :]), axis=0
    )
    inputs = samples.astype(jnp.float32)
    return (inputs * blended + inputs).astype(jnp.bfloat16)


def solution(mesh):
    placed = (
        P("batch", "width"),
        P("width", None, None),
        P(None, None, "width"),
        P("width", None),
        P(None, "width"),
    )
    return jax.shard_map(
        shards, mesh=mesh, in_specs=placed, out_specs=P("batch", "width"), check_vma=False
    )
```

profile of v0, /device:TPU:0, one launch (start us, length us, event | category | flops | bytes accessed | tf_op | source)
XLA Modules:
  0.0 110.1 jit_solution(5122312011810263512)
XLA Ops:
  6.5 0.0 copy-start
  6.5 0.0 copy-start.1
  6.5 0.0 reduce-scatter.2.cloned.1.call-start
  6.5 8.0 %fusion.7 = f32[1024,2,256]{0,2,1:T(8,128)} fusion(bf16[2048,2,1024]{2,1,0:T(2,128)(2,1)} %param.6, bf16[256,2048]{1,0:T(8,128)(2,1)} %param.5), kind=kOutput, calls=%fused_computation.7 | convolution fusion | flops 2147483648 | bytes 11534336 | tf_op jit(solution)/shard_map/fek,bf->keb/dot_general | solution.py:11
  14.6 0.0 copy-start.2
  14.6 0.0 reduce-scatter.2.cloned.1.call-update
  14.6 0.0 all-gather.2.cloned.1.call-start
  14.6 46.5 %reduce-scatter.2.cloned.1.call-done = f32[256,2,256]{0,2,1:T(8,128)} async-done(((f32[1024,2,256]{0,2,1:T(8,128)}), f32[256,2,256]{0,2,1:T(8,128)}) %reduce-scatter.2.cloned.1.call-update) | async-done | bytes 524304 | tf_op jit(solution)/shard_map/reduce_scatter | solution.py:10
  61.1 1.8 %tanh_convert_fusion = bf16[256,2,256]{0,2,1:T(8,128)(2,1)} fusion(f32[256,2,256]{0,2,1:T(8,128)} %reduce-scatter.2.cloned.1.call-done), kind=kLoop, calls=%fused_computation.9 | loop fusion | flops 131072 | bytes 786432 | tf_op jit(solution)/shard_map/convert_element_type | solution.py:16
  62.9 0.0 all-gather.2.cloned.1.call-update
  62.9 0.0 copy-done
  62.9 0.0 copy-done.1
  63.0 0.4 fusion.11
  63.3 10.2 %psum.7 = f32[256,2]{0,1:T(2,128)S(1)} all-reduce(f32[256,2]{0,1:T(2,128)S(1)} %fusion.11), channel_id=1, replica_groups=mesh['batch'=8,'width'=4] {'width'}, use_global_device_ids=true, to_apply=%region_0.0 | all-reduce | flops 512 | bytes 4096 | tf_op jit(solution)/shard_map/psum | solution.py:8
  73.6 18.7 %all-gather.2.cloned.1.call-done = bf16[1024,2,256]{0,2,1:T(8,128)(2,1)} async-done(((bf16[256,2,256]{0,2,1:T(8,128)(2,1)}), bf16[1024,2,256]{0,2,1:T(8,128)(2,1)}) %all-gather.2.cloned.1.call-update) | async-done | bytes 1048592 | tf_op jit(solution)/shard_map/all_gather | solution.py:19
  92.2 0.0 copy-done.2
  92.2 9.7 %multiply_reduce_fusion = f32[256,2048]{1,0:T(8,128)S(1)} fusion(bf16[1024,2,256]{0,2,1:T(8,128)(2,1)} %all-gather.2.cloned.1.call-done, bf16[1024,2,2048]{2,1,0:T(2,128)(2,1)} %param.7, f32[2,2048]{1,0:T(2,128)S(1)} %copy-done.2, f32[2,256]{1,0:T(2,128)S(1)} %divide_bitcast_fusion), kind=kOutput, calls=%fused_computation.4 | convolution fusion | flops 2150105088 | bytes 11552768 | tf_op jit(solution)/shard_map/keb,kef->ebf/dot_general | solution.py:17
  102.0 1.3 %fusion.6 = bf16[256,2048]{1,0:T(8,128)(2,1)} fusion(f32[256,2048]{1,0:T(8,128)S(1)} %multiply_reduce_fusion, bf16[256,2048]{1,0:T(8,128)(2,1)S(1)} %copy-done.1), kind=kLoop, calls=%fused_computation.6 | loop fusion | flops 2097152 | bytes 4194304 | tf_op jit(solution)/shard_map/convert_element_type | solution.py:27
  (1 shorter events, 0.0 us)
Async XLA Ops:
  6.5 56.4 %copy-start = (bf16[2048,2]{0,1:T(2,128)(2,1)S(1)}, bf16[2048,2]{0,1:T(2,128)(2,1)}, u32[]{:S(2)}) copy-start(bf16[2048,2]{0,1:T(2,128)(2,1)} %param.8) | copy-start | bytes 24580
  6.5 56.4 %copy-start.1 = (bf16[256,2048]{1,0:T(8,128)(2,1)S(1)}, bf16[256,2048]{1,0:T(8,128)(2,1)}, u32[]{:S(2)}) copy-start(bf16[256,2048]{1,0:T(8,128)(2,1)} %param.5) | copy-start | bytes 3145732
  6.5 54.6 %reduce-scatter.2.cloned.1.call-start = ((), (), s32[]{:S(2)}) async-start(), calls=%async_computation.1 | async-start | bytes 2621440 | tf_op jit(solution)/shard_map/reduce_scatter | solution.py:10
  14.6 77.7 %copy-start.2 = (f32[2,2048]{1,0:T(2,128)S(1)}, f32[2,2048]{1,0:T(2,128)}, u32[]{:S(2)}) copy-start(f32[2,2048]{1,0:T(2,128)} %param.9) | copy-start | bytes 49156
  14.6 77.6 %all-gather.2.cloned.1.call-start = ((), (), s32[]{:S(2)}) async-start(), calls=%async_computation.2 | async-start | bytes 1310720 | tf_op jit(solution)/shard_map/all_gather | solution.py:19
Sparse Core Ops, SparseCore 0:
  14.7 46.3 reduce-scatter.1
  63.1 29.1 all-gather.1
where the time goes:
time: 110 us
  waiting for transfers between devices  65.1 us (59%)
  matrix products  18.1 us (16%)
  between operations  13.4 us (12%)
  blocking collectives  10.2 us (9%)
  other arithmetic  3.15 us (3%)
    reduce_scatter x1, waiting for transfers between devices, shards(): lax.psum_scatter(jnp.einsum('fek,bf->keb', rank_down, samples, preferred_...  46.5 us
    all_gather x1, waiting for transfers between devices, shards(): lax.all_gather(hidden_share, 'width', axis=0, tiled=True)  18.7 us
    psum x1, blocking collectives, shards(): lax.psum(jnp.dot(samples, gate_proj, preferred_element_type=jnp.float32),...  10.2 us
    dot_general x1, matrix products, shards(): jnp.einsum('keb,kef->ebf', lax.all_gather(hidden_share, 'width', axis=0,...  9.73 us
    dot_general x1, matrix products, shards(): jnp.einsum('fek,bf->keb', rank_down, samples, preferred_element_type=jnp....  8.02 us
  transfers between devices with their start and end apart: 2, of which 2 were waited for; matrix products, arithmetic and copies ran while one was open for 0% of the time, Pallas kernels for 0%

commit v1 on v0

v1 whole, which is shorter than its diff:
```python
import jax
import jax.numpy as jnp
from jax import lax
from jax.sharding import PartitionSpec as P


def span(masks):
    out = [0]
    for m in masks:
        out = out + [s ^ m for s in out]
    return out


def swap(value, mask, size):
    return lax.ppermute(value, "width", [(i, i ^ mask) for i in range(size)])


def shards(samples, rank_down, rank_up, gate_proj, expert_bias):
    size = lax.axis_size("width")
    me = lax.axis_index("width")
    experts, rank = rank_down.shape[1:]
    masks = [(2 << i) - 1 for i in range(size.bit_length() - 1)]

    logits = jnp.transpose(jnp.dot(samples, gate_proj, preferred_element_type=jnp.float32))
    for m in masks:
        logits = logits + swap(logits, m, size)
    gating = jax.nn.sigmoid(logits)

    partial = jnp.einsum("bf,fek->ebk", samples, rank_down, preferred_element_type=jnp.float32)
    share = rank // size
    hidden = []
    for e in range(experts):
        order = masks if e % 2 == 0 else masks[::-1]
        held = {
            r: lax.dynamic_slice_in_dim(partial[e], (me ^ r) * share, share, axis=1)
            for r in range(size)
        }
        for i, m in enumerate(order):
            rest = span(order[i + 1 :])
            got = swap(jnp.stack([held[m ^ s] for s in rest]).astype(jnp.bfloat16), m, size)
            held = {s: held[s] + got[j].astype(jnp.float32) for j, s in enumerate(rest)}
        names, have = [0], jnp.tanh(held[0]).astype(jnp.bfloat16)[None]
        for m in order[::-1]:
            names, have = names + [s ^ m for s in names], jnp.concatenate([have, swap(have, m, size)])
        place = jnp.array([names.index(r) for r in range(size)])
        hidden.append(
            jnp.concatenate(
                [lax.dynamic_index_in_dim(have, place[me ^ q], 0, keepdims=False) for q in range(size)], axis=1
            )
        )
    expanded = jnp.einsum("ebk,kef->ebf", jnp.stack(hidden), rank_up, preferred_element_type=jnp.float32)
    blended = jnp.sum(gating[:, :, None] * (expanded + expert_bias[:, None, :]), axis=0)
    inputs = samples.astype(jnp.float32)
    return (inputs * blended + inputs).astype(jnp.bfloat16)


def solution(mesh):
    placed = (
        P("batch", "width"),
        P("width", None, None),
        P(None, None, "width"),
        P("width", None),
        P(None, "width"),
    )
    return jax.shard_map(
        shards, mesh=mesh, in_specs=placed, out_specs=P("batch", "width"), check_vma=False
    )
```

time: 110 us -> 81.2 us (0.74)
  waiting for transfers between devices: 65.1 us -> 21 us
  starting transfers between devices: 0.04 us -> 19.4 us
  blocking collectives: 10.2 us -> 0 us
  between operations: 13.4 us -> 15.5 us
  other arithmetic: 3.15 us -> 5.06 us
  local copies, waits for them, and re-layouts: 0.01 us -> 1.81 us
    reduce_scatter x1 -> x0, waiting for transfers between devices: 46.5 us -> none  [shards(): lax.psum_scatter(jnp.einsum('fek,bf->keb', rank_down, samples, preferred_...]
    ppermute x0 -> x10, waiting for transfers between devices: none -> 21 us  [swap(): return lax.ppermute(value, 'width', [(i, i ^ mask) for i in range(size)])]
    ppermute x0 -> x10, starting transfers between devices: none -> 19.4 us  [swap(): return lax.ppermute(value, 'width', [(i, i ^ mask) for i in range(size)])]
    all_gather x1 -> x0, waiting for transfers between devices: 18.7 us -> none  [shards(): lax.all_gather(hidden_share, 'width', axis=0, tiled=True)]
    psum x1 -> x0, blocking collectives: 10.2 us -> none  [shards(): lax.psum(jnp.dot(samples, gate_proj, preferred_element_type=jnp.float32),...]
    dynamic_slice x0 -> x11, local copies, waits for them, and re-layouts: none -> 1.58 us  [the longest x10 0.89 us: shards(): lax.dynamic_index_in_dim(have, place[me ^ q], 0, keepdims=False)]
    another operation x0 -> x4, other arithmetic: none -> 1.57 us  [the longest x2 1.46 us: shards(): jnp.stack([held[m ^ s] for s in rest]).astype(jnp.bfloat16)]
  transfers between devices with their start and end apart: 2 -> 10, of which waited for: 2 -> 6; matrix products, arithmetic and copies ran while one was open for 0% -> 5% of each run, Pallas kernels for 0% -> 0%
where the time goes in v1:
time: 81.2 us; the launch traced here: 80.8 us
  waiting for transfers between devices  21 us (26%)
  starting transfers between devices  19.4 us (24%)
  matrix products  18 us (22%)
  between operations  15.5 us (19%)
  other arithmetic  5.06 us (6%)
  local copies, waits for them, and re-layouts  1.81 us (2%)
    ppermute x10, waiting for transfers between devices, swap(): return lax.ppermute(value, 'width', [(i, i ^ mask) for i in range(size)])  21 us
    ppermute x10, starting transfers between devices, swap(): return lax.ppermute(value, 'width', [(i, i ^ mask) for i in range(size)])  19.4 us
    dot_general x1, matrix products, shards(): jnp.einsum('ebk,kef->ebf', jnp.stack(hidden), rank_up, preferred_element_...  9.31 us
    dot_general x1, matrix products, shards(): jnp.einsum('bf,fek->ebk', samples, rank_down, preferred_element_type=jnp....  8.36 us
  transfers between devices with their start and end apart: 10, of which 6 were waited for; matrix products, arithmetic and copies ran while one was open for 5% of the time, Pallas kernels for 0%

profile of v1, /device:TPU:0, one launch (start us, length us, event | category | flops | bytes accessed | tf_op | source)
XLA Modules:
  0.0 80.8 jit_solution(9664080090790069509)
XLA Ops:
  0.0 8.4 %fusion.7 = f32[2,256,1024]{1,2,0:T(8,128)S(1)} fusion(bf16[2048,2,1024]{2,1,0:T(2,128)(2,1)} %param.8, bf16[256,2048]{1,0:T(8,128)(2,1)} %param.7), kind=kOutput, calls=%fused_computation.7 | convolution fusion | flops 2147483648 | bytes 11534336 | tf_op jit(solution)/shard_map/bf,fek->ebk/dot_general | solution.py:29
  8.4 0.0 copy-start.1
  8.4 0.0 copy-start.2
  8.4 0.0 copy-start.3
  8.4 0.1 fusion.15
  8.6 0.7 pad_maximum_fusion.4
  9.3 5.1 %collective-permute-start.6 = (bf16[2,256,256]{1,2,0:T(8,128)(2,1)}, bf16[2,256,256]{1,2,0:T(8,128)(2,1)S(1)}, u32[]{:S(2)}, u32[]{:S(2)}) collective-permute-start(bf16[2,256,256]{1,2,0:T(8,128)(2,1)} %pad_maximum_fusion.4), channel_id=1, source_target_pairs={{0,3},{1,2},{2,1},{3,0},{4,7},{5,6},{6,5},{7,4},{8,11},{9,10},{10,... | collective-permute-start | bytes 786440 | tf_op jit(solution)/shard_map/ppermute | solution.py:15
  14.4 0.7 pad_maximum_fusion.2
  15.2 0.0 collective-permute-start.2
  15.2 6.7 %collective-permute-done.6 = bf16[2,256,256]{1,2,0:T(8,128)(2,1)S(1)} collective-permute-done((bf16[2,256,256]{1,2,0:T(8,128)(2,1)}, bf16[2,256,256]{1,2,0:T(8,128)(2,1)S(1)}, u32[]{:S(2)}, u32[]{:S(2)}) %collective-permute-start.6) | collective-permute-done | bytes 262176 | tf_op jit(solution)/shard_map/ppermute | solution.py:15
  21.9 4.5 %collective-permute-start.7 = (bf16[1,256,256]{1,2,0:T(8,128)(2,1)S(1)}, bf16[1,256,256]{1,2,0:T(8,128)(2,1)S(1)}, u32[]{:S(2)}, u32[]{:S(2)}) collective-permute-start(bf16[1,256,256]{1,2,0:T(8,128)(2,1)S(1)} %add_convert_fusion), channel_id=1, source_target_pairs={{0,1},{1,0},{2,3},{3,2},{4,5},{5,4},{6,7},{7,6},{8,9},{9,8},{10,11... | collective-permute-start | bytes 393224 | tf_op jit(solution)/shard_map/ppermute | solution.py:15
  26.4 0.5 collective-permute-done.2
  26.8 0.9 %add_convert_fusion.1 = bf16[1,256,256]{1,2,0:T(8,128)(2,1)S(1)} fusion(f32[1,256,1024]{1,2,0:T(8,128)S(1)} %get-tuple-element.5, s32[]{:T(128)S(6)} %select_n.60, bf16[2,256,256]{1,2,0:T(8,128)(2,1)} %collective-permute-done.2), kind=kLoop, calls=%fused_computation.25 | loop fusion | flops 196608 | bytes 524292 | tf_op jit(solution)/shard_map/convert_element_type | solution.py:40
  27.8 2.7 %collective-permute-start.3 = (bf16[1,256,256]{1,2,0:T(8,128)(2,1)S(1)}, bf16[1,256,256]{1,2,0:T(8,128)(2,1)S(1)}, u32[]{:S(2)}, u32[]{:S(2)}) collective-permute-start(bf16[1,256,256]{1,2,0:T(8,128)(2,1)S(1)} %add_convert_fusion.1), channel_id=1, source_target_pairs={{0,3},{1,2},{2,1},{3,0},{4,7},{5,6},{6,5},{7,4},{8,11},{9,10},{10,... | collective-permute-start | bytes 393224 | tf_op jit(solution)/shard_map/ppermute | solution.py:15
  30.4 0.0 collective-permute-done.7
  30.4 0.1 tanh_convert_fusion
  30.5 1.0 %collective-permute-start.8 = (bf16[1,256,256]{1,2,0:T(8,128)(2,1)S(1)}, bf16[1,256,256]{1,2,0:T(8,128)(2,1)S(1)}, u32[]{:S(2)}, u32[]{:S(2)}) collective-permute-start(bf16[1,256,256]{1,2,0:T(8,128)(2,1)S(1)} %tanh_convert_fusion), channel_id=1, source_target_pairs={{0,1},{1,0},{2,3},{3,2},{4,5},{5,4},{6,7},{7,6},{8,9},{9,8},{10,11... | collective-permute-start | bytes 393224 | tf_op jit(solution)/shard_map/ppermute | solution.py:15
  31.5 4.6 %collective-permute-done.3 = bf16[1,256,256]{1,2,0:T(8,128)(2,1)S(1)} collective-permute-done((bf16[1,256,256]{1,2,0:T(8,128)(2,1)S(1)}, bf16[1,256,256]{1,2,0:T(8,128)(2,1)S(1)}, u32[]{:S(2)}, u32[]{:S(2)}) %collective-permute-start.3) | collective-permute-done | bytes 131104 | tf_op jit(solution)/shard_map/ppermute | solution.py:15
  36.0 1.0 %tanh_convert_fusion.1 = bf16[1,256,256]{1,2,0:T(8,128)(2,1)S(1)} fusion(bf16[1,256,256]{1,2,0:T(8,128)(2,1)S(1)} %collective-permute-done.3, f32[1,256,1024]{1,2,0:T(8,128)S(1)} %get-tuple-element.5, s32[]{:T(128)S(6)} %select_n.57, bf16[2,256,256]{1,2,0:T(8,128)(2,1)} %collective-permute-done.2), kind=kLoop, calls=%fused_computation.24 | loop fusion | flops 327680 | bytes 655364 | tf_op jit(solution)/shard_map/convert_element_type | solution.py:42
  37.0 2.0 %collective-permute-start.4 = (bf16[1,256,256]{1,2,0:T(8,128)(2,1)S(1)}, bf16[1,256,256]{1,2,0:T(8,128)(2,1)S(1)}, u32[]{:S(2)}, u32[]{:S(2)}) collective-permute-start(bf16[1,256,256]{1,2,0:T(8,128)(2,1)S(1)} %tanh_convert_fusion.1), channel_id=1, source_target_pairs={{0,3},{1,2},{2,1},{3,0},{4,7},{5,6},{6,5},{7,4},{8,11},{9,10},{10,... | collective-permute-start | bytes 393224 | tf_op jit(solution)/shard_map/ppermute | solution.py:15
  39.0 0.4 fusion.18
  39.3 0.0 collective-permute-start
  39.3 0.0 copy-done.3
  39.4 0.7 fusion.16
  55.3 0.0 collective-permute-done
  55.3 2.7 %collective-permute-start.1 = (f32[2,256]{1,0:T(2,128)S(1)}, f32[2,256]{1,0:T(2,128)S(1)}, u32[]{:S(2)}, u32[]{:S(2)}) collective-permute-start(f32[2,256]{1,0:T(2,128)S(1)} %add.101), channel_id=1, source_target_pairs={{0,3},{1,2},{2,1},{3,0},{4,7},{5,6},{6,5},{7,4},{8,11},{9,10},{10,... | collective-permute-start | bytes 6152 | tf_op jit(solution)/shard_map/ppermute | solution.py:15
  58.0 0.0 collective-permute-done.8
  58.1 1.3 %collective-permute-start.9 = (bf16[2,256,256]{1,2,0:T(8,128)(2,1)S(1)}, bf16[2,256,256]{1,2,0:T(8,128)(2,1)S(1)}, u32[]{:S(2)}, u32[]{:S(2)}) collective-permute-start(bf16[2,256,256]{1,2,0:T(8,128)(2,1)S(1)} %pad_maximum_fusion.5), channel_id=1, source_target_pairs={{0,3},{1,2},{2,1},{3,0},{4,7},{5,6},{6,5},{7,4},{8,11},{9,10},{10,... | collective-permute-start | bytes 786440 | tf_op jit(solution)/shard_map/ppermute | solution.py:15
  59.3 0.0 collective-permute-done.4
  59.4 0.3 collective-permute-start.5
  59.6 1.2 %collective-permute-done.1 = f32[2,256]{1,0:T(2,128)S(1)} collective-permute-done((f32[2,256]{1,0:T(2,128)S(1)}, f32[2,256]{1,0:T(2,128)S(1)}, u32[]{:S(2)}, u32[]{:S(2)}) %collective-permute-start.1) | collective-permute-done | bytes 2080 | tf_op jit(solution)/shard_map/ppermute | solution.py:15
  60.9 0.0 copy-start.4
  60.9 7.0 %collective-permute-done.9 = bf16[2,256,256]{1,2,0:T(8,128)(2,1)S(1)} collective-permute-done((bf16[2,256,256]{1,2,0:T(8,128)(2,1)S(1)}, bf16[2,256,256]{1,2,0:T(8,128)(2,1)S(1)}, u32[]{:S(2)}, u32[]{:S(2)}) %collective-permute-start.9) | collective-permute-done | bytes 262176 | tf_op jit(solution)/shard_map/ppermute | solution.py:15
  67.9 0.1 pad_maximum_fusion.1
  68.0 0.1 copy.18
  68.1 0.1 copy.17
  68.2 0.1 copy.16
  68.3 0.1 copy.15
  68.4 1.1 %collective-permute-done.5 = bf16[2,256,256]{1,2,0:T(8,128)(2,1)S(1)} collective-permute-done((bf16[2,256,256]{1,2,0:T(8,128)(2,1)S(1)}, bf16[2,256,256]{1,2,0:T(8,128)(2,1)S(1)}, u32[]{:S(2)}, u32[]{:S(2)}) %collective-permute-start.5) | collective-permute-done | bytes 262176 | tf_op jit(solution)/shard_map/ppermute | solution.py:15
  69.5 0.1 pad_maximum_fusion
  69.6 0.1 copy.14
  69.7 0.1 copy.13
  69.8 0.1 copy.12
  69.9 0.1 copy.11
  70.0 0.1 maximum_bitcast_fusion.1
  70.1 0.1 maximum_bitcast_fusion
  70.2 9.3 %multiply_reduce_fusion = f32[256,2048]{1,0:T(8,128)S(1)} fusion(bf16[1024,2,2048]{2,1,0:T(2,128)(2,1)} %param.9, f32[2,2048]{1,0:T(2,128)S(1)} %copy-done.4, f32[2,256]{1,0:T(2,128)S(1)} %add_divide_fusion, bf16[1,256,1024]{2,1,0:T(8,128)(2,1)S(1)} %maximum_bitcast_fusion.1, bf16[1,256,1024]{2,1,0:T(8,128)(2,1)S(1)} %maximum_bitcast_fusion), kind=kOutput, calls=%fused_computation.4 | convolution fusion | flops 2150629376 | bytes 11552768 | tf_op jit(solution)/shard_map/ebk,kef->ebf/dot_general | solution.py:51
  79.5 1.3 %fusion.6 = bf16[256,2048]{1,0:T(8,128)(2,1)} fusion(f32[256,2048]{1,0:T(8,128)S(1)} %multiply_reduce_fusion, bf16[256,2048]{1,0:T(8,128)(2,1)S(1)} %copy-done.1), kind=kLoop, calls=%fused_computation.6 | loop fusion | flops 2097152 | bytes 4194304 | tf_op jit(solution)/shard_map/convert_element_type | solution.py:54
  (14 shorter events, 0.3 us)
Async XLA Ops:
  0.0 39.0 %copy-start = (bf16[2048,2]{0,1:T(2,128)(2,1)S(1)}, bf16[2048,2]{0,1:T(2,128)(2,1)}, u32[]{:S(2)}) copy-start(bf16[2048,2]{0,1:T(2,128)(2,1)} %param.10) | copy-start | bytes 24580
  8.4 30.6 %copy-start.1 = (bf16[256,2048]{1,0:T(8,128)(2,1)S(1)}, bf16[256,2048]{1,0:T(8,128)(2,1)}, u32[]{:S(2)}) copy-start(bf16[256,2048]{1,0:T(8,128)(2,1)} %param.7) | copy-start | bytes 3145732
  8.4 31.0 %copy-start.2 = (s32[4]{0:T(128)S(1)}, s32[4]{0:T(128)}, u32[]{:S(2)}) copy-start(s32[4]{0:T(128)} %constant.52.clone) | copy-start | bytes 52
  8.4 31.0 %copy-start.3 = (s32[4]{0:T(128)S(1)}, s32[4]{0:T(128)}, u32[]{:S(2)}) copy-start(s32[4]{0:T(128)} %constant.53.clone) | copy-start | bytes 52
  9.3 12.5 %collective-permute-start.6 = (bf16[2,256,256]{1,2,0:T(8,128)(2,1)}, bf16[2,256,256]{1,2,0:T(8,128)(2,1)S(1)}, u32[]{:S(2)}, u32[]{:S(2)}) collective-permute-start(bf16[2,256,256]{1,2,0:T(8,128)(2,1)} %pad_maximum_fusion.4), channel_id=1, source_target_pairs={{0,3},{1,2},{2,1},{3,0},{4,7},{5,6},{6,5},{7,4},{8,11},{9,10},{10,... | collective-permute-start | bytes 786440 | tf_op jit(solution)/shard_map/ppermute | solution.py:15
  15.2 11.7 %collective-permute-start.2 = (bf16[2,256,256]{1,2,0:T(8,128)(2,1)}, bf16[2,256,256]{1,2,0:T(8,128)(2,1)}, u32[]{:S(2)}, u32[]{:S(2)}) collective-permute-start(bf16[2,256,256]{1,2,0:T(8,128)(2,1)} %pad_maximum_fusion.2), channel_id=1, source_target_pairs={{0,1},{1,0},{2,3},{3,2},{4,5},{5,4},{6,7},{7,6},{8,9},{9,8},{10,11... | collective-permute-start | bytes 786440 | tf_op jit(solution)/shard_map/ppermute | solution.py:15
  21.9 8.6 %collective-permute-start.7 = (bf16[1,256,256]{1,2,0:T(8,128)(2,1)S(1)}, bf16[1,256,256]{1,2,0:T(8,128)(2,1)S(1)}, u32[]{:S(2)}, u32[]{:S(2)}) collective-permute-start(bf16[1,256,256]{1,2,0:T(8,128)(2,1)S(1)} %add_convert_fusion), channel_id=1, source_target_pairs={{0,1},{1,0},{2,3},{3,2},{4,5},{5,4},{6,7},{7,6},{8,9},{9,8},{10,11... | collective-permute-start | bytes 393224 | tf_op jit(solution)/shard_map/ppermute | solution.py:15
  27.8 8.2 %collective-permute-start.3 = (bf16[1,256,256]{1,2,0:T(8,128)(2,1)S(1)}, bf16[1,256,256]{1,2,0:T(8,128)(2,1)S(1)}, u32[]{:S(2)}, u32[]{:S(2)}) collective-permute-start(bf16[1,256,256]{1,2,0:T(8,128)(2,1)S(1)} %add_convert_fusion.1), channel_id=1, source_target_pairs={{0,3},{1,2},{2,1},{3,0},{4,7},{5,6},{6,5},{7,4},{8,11},{9,10},{10,... | collective-permute-start | bytes 393224 | tf_op jit(solution)/shard_map/ppermute | solution.py:15
  30.5 27.5 %collective-permute-start.8 = (bf16[1,256,256]{1,2,0:T(8,128)(2,1)S(1)}, bf16[1,256,256]{1,2,0:T(8,128)(2,1)S(1)}, u32[]{:S(2)}, u32[]{:S(2)}) collective-permute-start(bf16[1,256,256]{1,2,0:T(8,128)(2,1)S(1)} %tanh_convert_fusion), channel_id=1, source_target_pairs={{0,1},{1,0},{2,3},{3,2},{4,5},{5,4},{6,7},{7,6},{8,9},{9,8},{10,11... | collective-permute-start | bytes 393224 | tf_op jit(solution)/shard_map/ppermute | solution.py:15
  37.0 22.3 %collective-permute-start.4 = (bf16[1,256,256]{1,2,0:T(8,128)(2,1)S(1)}, bf16[1,256,256]{1,2,0:T(8,128)(2,1)S(1)}, u32[]{:S(2)}, u32[]{:S(2)}) collective-permute-start(bf16[1,256,256]{1,2,0:T(8,128)(2,1)S(1)} %tanh_convert_fusion.1), channel_id=1, source_target_pairs={{0,3},{1,2},{2,1},{3,0},{4,7},{5,6},{6,5},{7,4},{8,11},{9,10},{10,... | collective-permute-start | bytes 393224 | tf_op jit(solution)/shard_map/ppermute | solution.py:15
  39.3 16.0 %collective-permute-start = (f32[2,256]{1,0:T(2,128)S(1)}, f32[2,256]{1,0:T(2,128)S(1)}, u32[]{:S(2)}, u32[]{:S(2)}) collective-permute-start(f32[2,256]{1,0:T(2,128)S(1)} %fusion.18), channel_id=1, source_target_pairs={{0,1},{1,0},{2,3},{3,2},{4,5},{5,4},{6,7},{7,6},{8,9},{9,8},{10,11... | collective-permute-start | bytes 6152 | tf_op jit(solution)/shard_map/ppermute | solution.py:15
  55.3 5.5 %collective-permute-start.1 = (f32[2,256]{1,0:T(2,128)S(1)}, f32[2,256]{1,0:T(2,128)S(1)}, u32[]{:S(2)}, u32[]{:S(2)}) collective-permute-start(f32[2,256]{1,0:T(2,128)S(1)} %add.101), channel_id=1, source_target_pairs={{0,3},{1,2},{2,1},{3,0},{4,7},{5,6},{6,5},{7,4},{8,11},{9,10},{10,... | collective-permute-start | bytes 6152 | tf_op jit(solution)/shard_map/ppermute | solution.py:15
  58.1 9.8 %collective-permute-start.9 = (bf16[2,256,256]{1,2,0:T(8,128)(2,1)S(1)}, bf16[2,256,256]{1,2,0:T(8,128)(2,1)S(1)}, u32[]{:S(2)}, u32[]{:S(2)}) collective-permute-start(bf16[2,256,256]{1,2,0:T(8,128)(2,1)S(1)} %pad_maximum_fusion.5), channel_id=1, source_target_pairs={{0,3},{1,2},{2,1},{3,0},{4,7},{5,6},{6,5},{7,4},{8,11},{9,10},{10,... | collective-permute-start | bytes 786440 | tf_op jit(solution)/shard_map/ppermute | solution.py:15
  59.4 10.1 %collective-permute-start.5 = (bf16[2,256,256]{1,2,0:T(8,128)(2,1)S(1)}, bf16[2,256,256]{1,2,0:T(8,128)(2,1)S(1)}, u32[]{:S(2)}, u32[]{:S(2)}) collective-permute-start(bf16[2,256,256]{1,2,0:T(8,128)(2,1)S(1)} %pad_maximum_fusion.3), channel_id=1, source_target_pairs={{0,1},{1,0},{2,3},{3,2},{4,5},{5,4},{6,7},{7,6},{8,9},{9,8},{10,11... | collective-permute-start | bytes 786440 | tf_op jit(solution)/shard_map/ppermute | solution.py:15
  60.9 9.3 %copy-start.4 = (f32[2,2048]{1,0:T(2,128)S(1)}, f32[2,2048]{1,0:T(2,128)}, u32[]{:S(2)}) copy-start(f32[2,2048]{1,0:T(2,128)} %param.11) | copy-start | bytes 49156

commit v2 on v0

v2 whole, which is shorter than its diff:
```python
import jax
import jax.numpy as jnp
from jax import lax
from jax.sharding import PartitionSpec as P


def swap(value, bit, size):
    return lax.ppermute(value, "width", [(i, i ^ bit) for i in range(size)])


def side(me, bit):
    return (me & bit) // bit


def half(value, which):
    n = value.shape[1] // 2
    return lax.dynamic_slice_in_dim(value, which * n, n, axis=1)


def hidden_of(partial, order, me, size):
    held = partial
    for bit in order[:-1]:
        mine = side(me, bit)
        got = swap(half(held, 1 - mine).astype(jnp.bfloat16), bit, size)
        held = half(held, mine) + got.astype(jnp.float32)
    for bit in order[-1:]:
        held = held + swap(held.astype(jnp.bfloat16), bit, size).astype(jnp.float32)
    return jnp.tanh(held).astype(jnp.bfloat16)


def shards(samples, rank_down, rank_up, gate_proj, expert_bias):
    size = lax.axis_size("width")
    me = lax.axis_index("width")
    experts = rank_down.shape[1]
    bits = [1 << i for i in range(size.bit_length() - 1)]

    partial = jnp.einsum("bf,fek->ebk", samples, rank_down, preferred_element_type=jnp.float32)
    logits = jnp.transpose(jnp.dot(samples, gate_proj, preferred_element_type=jnp.float32))
    up = jnp.transpose(rank_up, (1, 0, 2))
    hidden = []
    for e in range(experts):
        order = bits if e % 2 == 0 else bits[::-1]
        have = hidden_of(partial[e], order, me, size)
        for bit in order[:-1][::-1]:
            got = swap(have, bit, size)
            first = side(me, bit) == 0
            have = jnp.concatenate([jnp.where(first, have, got), jnp.where(first, got, have)], axis=1)
        hidden.append(have)
    for bit in bits:
        logits = logits + swap(logits, bit, size)
    gating = jax.nn.sigmoid(logits)
    blended = sum(
        gating[e][:, None]
        * (jnp.dot(hidden[e], up[e], preferred_element_type=jnp.float32) + expert_bias[e][None])
        for e in range(experts)
    )
    inputs = samples.astype(jnp.float32)
    return (inputs * blended + inputs).astype(jnp.bfloat16)


def solution(mesh):
    placed = (
        P("batch", "width"),
        P("width", None, None),
        P(None, None, "width"),
        P("width", None),
        P(None, "width"),
    )
    return jax.shard_map(
        shards, mesh=mesh, in_specs=placed, out_specs=P("batch", "width"), check_vma=False
    )
```

time: 110 us -> 62.7 us (0.57)
  waiting for transfers between devices: 65.1 us -> 26 us
  between operations: 13.4 us -> 0.16 us
  local copies, waits for them, and re-layouts: 0.01 us -> 11.5 us
  blocking collectives: 10.2 us -> 0 us
  starting transfers between devices: 0.04 us -> 8.34 us
  other arithmetic: 3.15 us -> 0.47 us
  matrix products: 18.1 us -> 16 us
    reduce_scatter x1 -> x0, waiting for transfers between devices: 46.5 us -> none  [shards(): lax.psum_scatter(jnp.einsum('fek,bf->keb', rank_down, samples, preferred_...]
    ppermute x0 -> x8, waiting for transfers between devices: none -> 26 us  [swap(): return lax.ppermute(value, 'width', [(i, i ^ bit) for i in range(size)])]
    all_gather x1 -> x0, waiting for transfers between devices: 18.7 us -> none  [shards(): lax.all_gather(hidden_share, 'width', axis=0, tiled=True)]
    unnamed x6 -> x11, local copies, waits for them, and re-layouts: 0.01 us -> 11.3 us
    psum x1 -> x0, blocking collectives: 10.2 us -> none  [shards(): lax.psum(jnp.dot(samples, gate_proj, preferred_element_type=jnp.float32),...]
    ppermute x0 -> x8, starting transfers between devices: none -> 8.34 us  [swap(): return lax.ppermute(value, 'width', [(i, i ^ bit) for i in range(size)])]
    dot_general x2 -> x3, matrix products: 17.7 us -> 14.4 us  [the longest x1 8.35 us: shards(): jnp.einsum('bf,fek->ebk', samples, rank_down, preferred_element_type=jnp....]
    convert_element_type x2 -> x4, other arithmetic: 3.14 us -> 0.37 us  [the longest x2 0.23 us: hidden_of(): return jnp.tanh(held).astype(jnp.bfloat16)]
  transfers between devices with their start and end apart: 2 -> 8, of which waited for: 2 -> 5; matrix products, arithmetic and copies ran while one was open for 0% -> 37% of each run, Pallas kernels for 0% -> 0%
where the time goes in v2:
time: 62.7 us; the launch traced here: 62.5 us
  waiting for transfers between devices  26 us (41%)
  matrix products  16 us (26%)
  local copies, waits for them, and re-layouts  11.5 us (18%)
  starting transfers between devices  8.34 us (13%)
    ppermute x8, waiting for transfers between devices, swap(): return lax.ppermute(value, 'width', [(i, i ^ bit) for i in range(size)])  26 us
    unnamed x11, local copies, waits for them, and re-layouts  11.3 us
    dot_general x1, matrix products, shards(): jnp.einsum('bf,fek->ebk', samples, rank_down, preferred_element_type=jnp....  8.35 us
    ppermute x8, starting transfers between devices, swap(): return lax.ppermute(value, 'width', [(i, i ^ bit) for i in range(size)])  8.34 us
    dot_general x2, matrix products, shards(): jnp.dot(hidden[e], up[e], preferred_element_type=jnp.float32)  6.1 us
    dot_general x1, matrix products, shards(): jnp.dot(samples, gate_proj, preferred_element_type=jnp.float32)  1.59 us
  transfers between devices with their start and end apart: 8, of which 5 were waited for; matrix products, arithmetic and copies ran while one was open for 37% of the time, Pallas kernels for 0%

profile of v2, /device:TPU:0, one launch (start us, length us, event | category | flops | bytes accessed | tf_op | source)
XLA Modules:
  0.0 62.5 jit_solution(57330108215593197)
XLA Ops:
  0.0 0.0 copy-start
  0.0 0.7 %copy-done = bf16[2048,2]{0,1:T(2,128)(2,1)S(1)} copy-done((bf16[2048,2]{0,1:T(2,128)(2,1)S(1)}, bf16[2048,2]{0,1:T(2,128)(2,1)}, u32[]{:S(2)}) %copy-start) | copy-done | bytes 8216
  0.7 1.6 %fusion.29 = f32[2,256]{1,0:T(2,128)S(1)} fusion(bf16[2048,2]{0,1:T(2,128)(2,1)S(1)} %copy-done, bf16[256,2048]{1,0:T(8,128)(2,1)} %param.5), kind=kOutput, calls=%fused_computation.42 | convolution fusion | flops 2097152 | bytes 1058816 | tf_op jit(solution)/shard_map/dot_general | solution.py:38
  2.3 3.1 %collective-permute-start = (f32[2,256]{1,0:T(2,128)S(1)}, f32[2,256]{1,0:T(2,128)S(1)}, u32[]{:S(2)}, u32[]{:S(2)}) collective-permute-start(f32[2,256]{1,0:T(2,128)S(1)} %fusion.29), channel_id=1, source_target_pairs={{0,1},{1,0},{2,3},{3,2},{4,5},{5,4},{6,7},{7,6},{8,9},{9,8},{10,11... | collective-permute-start | bytes 6152 | tf_op jit(solution)/shard_map/ppermute | solution.py:8
  5.4 8.3 %fusion.10 = f32[2,256,1024]{1,2,0:T(8,128)S(1)} fusion(bf16[2048,2,1024]{2,1,0:T(2,128)(2,1)} %param.6, bf16[256,2048]{1,0:T(8,128)(2,1)} %param.5), kind=kOutput, calls=%fused_computation.14 | convolution fusion | flops 2147483648 | bytes 11534336 | tf_op jit(solution)/shard_map/bf,fek->ebk/dot_general | solution.py:37
  13.7 0.0 copy-start.2
  13.7 0.1 fusion.26
  13.9 2.7 %collective-permute-start.5 = (bf16[256,512]{0,1:T(8,128)(2,1)S(1)}, bf16[256,512]{0,1:T(8,128)(2,1)S(1)}, u32[]{:S(2)}, u32[]{:S(2)}) collective-permute-start(bf16[256,512]{0,1:T(8,128)(2,1)S(1)} %fusion.23), channel_id=1, source_target_pairs={{0,2},{1,3},{2,0},{3,1},{4,6},{5,7},{6,4},{7,5},{8,10},{9,11},{10,... | collective-permute-start | bytes 786440 | tf_op jit(solution)/shard_map/ppermute | solution.py:8
  16.6 0.5 collective-permute-start.2
  17.1 0.0 copy-done.2
  17.2 10.5 %copy.14 = bf16[1024,2,2048]{2,0,1:T(8,128)(2,1)} copy(bf16[1024,2,2048]{2,1,0:T(2,128)(2,1)} %param.7) | data formatting | bytes 16777216 | tf_op args[2]
  27.7 0.0 collective-permute-done
  27.7 0.0 collective-permute-start.1
  27.7 0.5 collective-permute-done.5
  28.2 0.1 fusion.21
  28.3 1.5 %collective-permute-start.6 = (bf16[256,512]{0,1:T(8,128)(2,1)S(1)}, bf16[256,512]{0,1:T(8,128)(2,1)S(1)}, u32[]{:S(2)}, u32[]{:S(2)}) collective-permute-start(bf16[256,512]{0,1:T(8,128)(2,1)S(1)} %fusion.21), channel_id=1, source_target_pairs={{0,1},{1,0},{2,3},{3,2},{4,5},{5,4},{6,7},{7,6},{8,9},{9,8},{10,11... | collective-permute-start | bytes 786440 | tf_op jit(solution)/shard_map/ppermute | solution.py:8
  29.7 2.5 %collective-permute-done.1 = f32[2,256]{1,0:T(2,128)S(1)} collective-permute-done((f32[2,256]{1,0:T(2,128)S(1)}, f32[2,256]{1,0:T(2,128)S(1)}, u32[]{:S(2)}, u32[]{:S(2)}) %collective-permute-start.1) | collective-permute-done | bytes 2080 | tf_op jit(solution)/shard_map/ppermute | solution.py:8
  32.3 0.0 collective-permute-done.2
  32.3 0.0 slice-start
  32.3 0.1 fusion.20
  32.4 0.1 collective-permute-start.3
  32.5 7.5 %collective-permute-done.6 = bf16[256,512]{0,1:T(8,128)(2,1)S(1)} collective-permute-done((bf16[256,512]{0,1:T(8,128)(2,1)S(1)}, bf16[256,512]{0,1:T(8,128)(2,1)S(1)}, u32[]{:S(2)}, u32[]{:S(2)}) %collective-permute-start.6) | collective-permute-done | bytes 262176 | tf_op jit(solution)/shard_map/ppermute | solution.py:8
  40.0 0.1 tanh_convert_fusion
  40.1 0.5 collective-permute-start.7
  40.6 12.1 %collective-permute-done.3 = bf16[256,512]{0,1:T(8,128)(2,1)S(1)} collective-permute-done((bf16[256,512]{0,1:T(8,128)(2,1)S(1)}, bf16[256,512]{0,1:T(8,128)(2,1)S(1)}, u32[]{:S(2)}, u32[]{:S(2)}) %collective-permute-start.3) | collective-permute-done | bytes 262176 | tf_op jit(solution)/shard_map/ppermute | solution.py:8
  52.7 0.1 tanh_convert_fusion.1
  52.8 0.1 collective-permute-start.4
  52.9 3.3 %collective-permute-done.7 = bf16[256,512]{0,1:T(8,128)(2,1)S(1)} collective-permute-done((bf16[256,512]{0,1:T(8,128)(2,1)S(1)}, bf16[256,512]{0,1:T(8,128)(2,1)S(1)}, u32[]{:S(2)}, u32[]{:S(2)}) %collective-permute-start.7) | collective-permute-done | bytes 262176 | tf_op jit(solution)/shard_map/ppermute | solution.py:8
  56.3 0.0 slice-start.1
  56.3 0.0 copy-start.1
  56.3 3.6 %fusion.6 = f32[256,2048]{1,0:T(8,128)S(1)} fusion(bf16[2,1024,2048]{2,1,0:T(8,128)(2,1)} %bitcast.50, f32[2048]{0:T(1024)S(1)} %bitcast.55, f32[256]{0:T(256)S(1)} %bitcast.57, bf16[256,512]{0,1:T(8,128)(2,1)S(1)} %get-tuple-element.10, bf16[256,512]{0,1:T(8,128)(2,1)S(1)} %get-tuple-element.9), kind=kOutput, calls=%fused_computation.10 | convolution fusion | flops 1075838976 | bytes 6824960 | tf_op jit(solution)/shard_map/dot_general | solution.py:54
  59.9 0.0 collective-permute-done.4
  60.0 0.0 slice-done
  60.0 0.0 slice-done.1
  60.0 0.0 copy-done.1
  60.0 2.5 %fusion.9 = bf16[256,2048]{1,0:T(8,128)(2,1)} fusion(f32[256,2048]{1,0:T(8,128)S(1)} %fusion.6, bf16[2,1024,2048]{2,1,0:T(8,128)(2,1)S(1)} %bitcast.53, bf16[256,2048]{1,0:T(8,128)(2,1)S(1)} %copy-done.1, f32[2048]{0:T(1024)S(1)} %bitcast.54, f32[256]{0:T(256)S(1)} %bitcast.56, bf16[256,512]{0,1:T(8,128)(2,1)S(1)} %get-tuple-element.8, ...), kind=kOutput, calls=%fused_computation.13 | convolution fusion | flops 1078460416 | bytes 8922112 | tf_op jit(solution)/shard_map/dot_general | solution.py:54
  (9 shorter events, 0.2 us)
Async XLA Ops:
  0.0 0.7 %copy-start = (bf16[2048,2]{0,1:T(2,128)(2,1)S(1)}, bf16[2048,2]{0,1:T(2,128)(2,1)}, u32[]{:S(2)}) copy-start(bf16[2048,2]{0,1:T(2,128)(2,1)} %param.8) | copy-start | bytes 24580
  2.3 25.4 %collective-permute-start = (f32[2,256]{1,0:T(2,128)S(1)}, f32[2,256]{1,0:T(2,128)S(1)}, u32[]{:S(2)}, u32[]{:S(2)}) collective-permute-start(f32[2,256]{1,0:T(2,128)S(1)} %fusion.29), channel_id=1, source_target_pairs={{0,1},{1,0},{2,3},{3,2},{4,5},{5,4},{6,7},{7,6},{8,9},{9,8},{10,11... | collective-permute-start | bytes 6152 | tf_op jit(solution)/shard_map/ppermute | solution.py:8
  13.7 3.4 %copy-start.2 = (f32[2,2048]{1,0:T(2,128)S(1)}, f32[2,2048]{1,0:T(2,128)}, u32[]{:S(2)}) copy-start(f32[2,2048]{1,0:T(2,128)} %param.9) | copy-start | bytes 49156
  13.9 14.3 %collective-permute-start.5 = (bf16[256,512]{0,1:T(8,128)(2,1)S(1)}, bf16[256,512]{0,1:T(8,128)(2,1)S(1)}, u32[]{:S(2)}, u32[]{:S(2)}) collective-permute-start(bf16[256,512]{0,1:T(8,128)(2,1)S(1)} %fusion.23), channel_id=1, source_target_pairs={{0,2},{1,3},{2,0},{3,1},{4,6},{5,7},{6,4},{7,5},{8,10},{9,11},{10,... | collective-permute-start | bytes 786440 | tf_op jit(solution)/shard_map/ppermute | solution.py:8
  16.6 15.7 %collective-permute-start.2 = (bf16[256,512]{0,1:T(8,128)(2,1)S(1)}, bf16[256,512]{0,1:T(8,128)(2,1)S(1)}, u32[]{:S(2)}, u32[]{:S(2)}) collective-permute-start(bf16[256,512]{0,1:T(8,128)(2,1)S(1)} %fusion.22), channel_id=1, source_target_pairs={{0,1},{1,0},{2,3},{3,2},{4,5},{5,4},{6,7},{7,6},{8,9},{9,8},{10,11... | collective-permute-start | bytes 786440 | tf_op jit(solution)/shard_map/ppermute | solution.py:8
  27.7 4.6 %collective-permute-start.1 = (f32[2,256]{1,0:T(2,128)S(1)}, f32[2,256]{1,0:T(2,128)S(1)}, u32[]{:S(2)}, u32[]{:S(2)}) collective-permute-start(f32[2,256]{1,0:T(2,128)S(1)} %add.61), channel_id=1, source_target_pairs={{0,2},{1,3},{2,0},{3,1},{4,6},{5,7},{6,4},{7,5},{8,10},{9,11},{10,... | collective-permute-start | bytes 6152 | tf_op jit(solution)/shard_map/ppermute | solution.py:8
  28.3 11.8 %collective-permute-start.6 = (bf16[256,512]{0,1:T(8,128)(2,1)S(1)}, bf16[256,512]{0,1:T(8,128)(2,1)S(1)}, u32[]{:S(2)}, u32[]{:S(2)}) collective-permute-start(bf16[256,512]{0,1:T(8,128)(2,1)S(1)} %fusion.21), channel_id=1, source_target_pairs={{0,1},{1,0},{2,3},{3,2},{4,5},{5,4},{6,7},{7,6},{8,9},{9,8},{10,11... | collective-permute-start | bytes 786440 | tf_op jit(solution)/shard_map/ppermute | solution.py:8
  32.3 27.7 %slice-start = ((s8[8388608]{0:T(1024)(128)(4,1)}), s8[4194304]{0:T(1024)(128)(4,1)S(1)}, s32[]{:S(2)}) async-start(s8[8388608]{0:T(1024)(128)(4,1)} %bitcast.51), calls=%async_computation | async-start | bytes 8388608
  32.4 20.3 %collective-permute-start.3 = (bf16[256,512]{0,1:T(8,128)(2,1)S(1)}, bf16[256,512]{0,1:T(8,128)(2,1)S(1)}, u32[]{:S(2)}, u32[]{:S(2)}) collective-permute-start(bf16[256,512]{0,1:T(8,128)(2,1)S(1)} %fusion.20), channel_id=1, source_target_pairs={{0,2},{1,3},{2,0},{3,1},{4,6},{5,7},{6,4},{7,5},{8,10},{9,11},{10,... | collective-permute-start | bytes 786440 | tf_op jit(solution)/shard_map/ppermute | solution.py:8
  40.1 16.1 %collective-permute-start.7 = (bf16[256,512]{0,1:T(8,128)(2,1)S(1)}, bf16[256,512]{0,1:T(8,128)(2,1)S(1)}, u32[]{:S(2)}, u32[]{:S(2)}) collective-permute-start(bf16[256,512]{0,1:T(8,128)(2,1)S(1)} %tanh_convert_fusion), channel_id=1, source_target_pairs={{0,2},{1,3},{2,0},{3,1},{4,6},{5,7},{6,4},{7,5},{8,10},{9,11},{10,... | collective-permute-start | bytes 786440 | tf_op jit(solution)/shard_map/ppermute | solution.py:8
  52.8 7.1 %collective-permute-start.4 = (bf16[256,512]{0,1:T(8,128)(2,1)S(1)}, bf16[256,512]{0,1:T(8,128)(2,1)S(1)}, u32[]{:S(2)}, u32[]{:S(2)}) collective-permute-start(bf16[256,512]{0,1:T(8,128)(2,1)S(1)} %tanh_convert_fusion.1), channel_id=1, source_target_pairs={{0,1},{1,0},{2,3},{3,2},{4,5},{5,4},{6,7},{7,6},{8,9},{9,8},{10,11... | collective-permute-start | bytes 786440 | tf_op jit(solution)/shard_map/ppermute | solution.py:8
  56.3 3.7 %slice-start.1 = ((s8[8388608]{0:T(1024)(128)(4,1)}), s8[4194304]{0:T(1024)(128)(4,1)S(1)}, s32[]{:S(2)}) async-start(s8[8388608]{0:T(1024)(128)(4,1)} %bitcast.51), calls=%async_computation.1 | async-start | bytes 8388608
  56.3 3.7 %copy-start.1 = (bf16[256,2048]{1,0:T(8,128)(2,1)S(1)}, bf16[256,2048]{1,0:T(8,128)(2,1)}, u32[]{:S(2)}) copy-start(bf16[256,2048]{1,0:T(8,128)(2,1)} %param.5) | copy-start | bytes 3145732

commit v3 on v0

v3 whole, which is shorter than its diff:
```python
import jax
import jax.numpy as jnp
from jax import lax
from jax.sharding import PartitionSpec as P

LANES = 128
BF16 = jnp.bfloat16
F32 = jnp.float32


def swap(value, bit, size):
    return lax.ppermute(value, "width", [(i, i ^ bit) for i in range(size)])


def half(value, which):
    n = value.shape[-1] // 2
    return lax.dynamic_slice_in_dim(value, which * n, n, axis=value.ndim - 1)


def shards(samples, rank_down, rank_up, gate_proj, expert_bias):
    size = lax.axis_size("width")
    me = lax.axis_index("width")
    experts, rank = rank_down.shape[1:]
    bits = [1 << i for i in range(size.bit_length() - 1)]
    orders = [bits, bits[::-1]]
    cut = rank // 2

    held = [
        jnp.einsum("bf,fek->ebk", samples, weights, preferred_element_type=F32)[:, :, -cut:]
        for weights in (rank_down[:, :, :cut], rank_down[:, :, cut - LANES :])
    ]
    logits = jnp.transpose(jnp.dot(samples, gate_proj, preferred_element_type=F32))
    held[0] = lax.optimization_barrier(held[0])
    logits, held[1] = lax.optimization_barrier((logits, held[1]))
    sent = [half(held[s], 1 - me // orders[s][0] % 2).astype(BF16) for s in range(2)]
    arrived = [swap(sent[s], orders[s][0], size) for s in range(2)]
    for bit in bits:
        logits = logits + swap(logits, bit, size)
    gate = jax.nn.sigmoid(logits)

    up = jnp.transpose(rank_up, (1, 0, 2))
    terms = []
    for s, order in enumerate(orders):
        total = half(held[s], me // order[0] % 2) + arrived[s].astype(F32)
        for bit in order[1:-1]:
            mine = me // bit % 2
            part = swap(half(total, 1 - mine).astype(BF16), bit, size)
            total = half(total, mine) + part.astype(F32)
        total = total + swap(total.astype(BF16), order[-1], size).astype(F32)
        have = jnp.tanh(total).astype(BF16)
        for bit in order[:-1][::-1]:
            part = swap(have, bit, size)
            low = me // bit % 2 == 0
            have = jnp.concatenate([jnp.where(low, have, part), jnp.where(low, part, have)], axis=2)
        for e in range(experts):
            terms.append(
                gate[e][:, None]
                * jnp.dot(have[e], up[e, s * cut : (s + 1) * cut], preferred_element_type=F32)
            )
    bias = sum(gate[e][:, None] * expert_bias[e][None] for e in range(experts))
    blended = sum(terms) + bias
    inputs = samples.astype(F32)
    return (inputs * blended + inputs).astype(BF16)


def solution(mesh):
    placed = (
        P("batch", "width"),
        P("width", None, None),
        P(None, None, "width"),
        P("width", None),
        P(None, "width"),
    )
    return jax.shard_map(
        shards, mesh=mesh, in_specs=placed, out_specs=P("batch", "width"), check_vma=False
    )
```

time: 110 us -> 60.6 us (0.55)
  waiting for transfers between devices: 65.1 us -> 22.9 us
  local copies, waits for them, and re-layouts: 0.01 us -> 14.6 us
  between operations: 13.4 us -> 0.16 us
  starting transfers between devices: 0.04 us -> 11 us
  blocking collectives: 10.2 us -> 0 us
  matrix products: 18.1 us -> 9.24 us
    reduce_scatter x1 -> x0, waiting for transfers between devices: 46.5 us -> none  [shards(): lax.psum_scatter(jnp.einsum('fek,bf->keb', rank_down, samples, preferred_...]
    ppermute x0 -> x8, waiting for transfers between devices: none -> 22.9 us  [swap(): return lax.ppermute(value, 'width', [(i, i ^ bit) for i in range(size)])]
    all_gather x1 -> x0, waiting for transfers between devices: 18.7 us -> none  [shards(): lax.all_gather(hidden_share, 'width', axis=0, tiled=True)]
    ppermute x0 -> x8, starting transfers between devices: none -> 11 us  [swap(): return lax.ppermute(value, 'width', [(i, i ^ bit) for i in range(size)])]
    unnamed x6 -> x9, local copies, waits for them, and re-layouts: 0.01 us -> 10.5 us
    psum x1 -> x0, blocking collectives: 10.2 us -> none  [shards(): lax.psum(jnp.dot(samples, gate_proj, preferred_element_type=jnp.float32),...]
    dot_general x3 -> x7, matrix products: 18.1 us -> 9.24 us  [the longest x4 5.93 us: shards(): jnp.dot(have[e], up[e, s * cut:(s + 1) * cut], preferred_element_type=F32)]
    slice x0 -> x7, local copies, waits for them, and re-layouts: none -> 2.61 us  [the longest x2 2.51 us: shards(): rank_down[:, :, :cut]]
  transfers between devices with their start and end apart: 2 -> 8, of which waited for: 2 -> 5; matrix products, arithmetic and copies ran while one was open for 0% -> 31% of each run, Pallas kernels for 0% -> 0%
where the time goes in v3:
time: 60.6 us; the launch traced here: 60.3 us
  waiting for transfers between devices  22.9 us (38%)
  local copies, waits for them, and re-layouts  14.6 us (24%)
  starting transfers between devices  11 us (18%)
  matrix products  9.24 us (15%)
  other arithmetic  2.39 us (4%)
    ppermute x8, waiting for transfers between devices, swap(): return lax.ppermute(value, 'width', [(i, i ^ bit) for i in range(size)])  22.9 us
    ppermute x8, starting transfers between devices, swap(): return lax.ppermute(value, 'width', [(i, i ^ bit) for i in range(size)])  11 us
    unnamed x9, local copies, waits for them, and re-layouts  10.5 us
    dot_general x4, matrix products, shards(): jnp.dot(have[e], up[e, s * cut:(s + 1) * cut], preferred_element_type=F32)  5.93 us
    dot_general x2, matrix products, shards(): jnp.einsum('bf,fek->ebk', samples, weights, preferred_element_type=F32)  2.94 us
    slice x2, local copies, waits for them, and re-layouts, shards(): rank_down[:, :, :cut]  2.51 us
    convert_element_type x2, local copies, waits for them, and re-layouts, shards(): half(held[s], 1 - me // orders[s][0] % 2).astype(BF16)  1.47 us
  transfers between devices with their start and end apart: 8, of which 5 were waited for; matrix products, arithmetic and copies ran while one was open for 31% of the time, Pallas kernels for 0%

profile of v3, /device:TPU:0, one launch (start us, length us, event | category | flops | bytes accessed | tf_op | source)
XLA Modules:
  0.0 60.3 jit_solution(14439916423054450415)
XLA Ops:
  0.0 0.0 copy-start
  0.0 0.0 slice-start
  0.0 0.0 copy-start.2
  0.0 2.5 %slice-done = bf16[2048,2,512]{2,1,0:T(2,128)(2,1)S(1)} async-done(((bf16[2048,2,1024]{2,1,0:T(2,128)(2,1)}), bf16[2048,2,512]{2,1,0:T(2,128)(2,1)S(1)}, s32[]{:S(2)}) %slice-start) | async-done | bytes 4194328 | tf_op jit(solution)/shard_map/slice | solution.py:30
  2.5 0.0 copy-done.2
  2.5 1.3 %fusion.12 = f32[2,256,512]{1,2,0:T(8,128)S(1)} fusion(bf16[2048,2,512]{2,1,0:T(2,128)(2,1)S(1)} %slice-done, bf16[256,2048]{1,0:T(8,128)(2,1)S(1)} %copy-done.2), kind=kOutput, calls=%fused_computation.20 | convolution fusion | flops 1073741824 | bytes 6291456 | tf_op jit(solution)/shard_map/bf,fek->ebk/dot_general | solution.py:29
  3.9 0.7 %dynamic-slice_convert_fusion.1 = bf16[2,256,256]{1,2,0:T(8,128)(2,1)} fusion(f32[2,256,512]{1,2,0:T(8,128)S(1)} %fusion.12, s32[]{:T(128)S(6)} %select_n.65), kind=kLoop, calls=%fused_computation.32 | loop fusion | bytes 524292 | tf_op jit(solution)/shard_map/convert_element_type | solution.py:35
  4.6 0.0 slice-start.1
  4.6 3.1 %collective-permute-start.2 = (bf16[2,256,256]{1,2,0:T(8,128)(2,1)}, bf16[2,256,256]{1,2,0:T(8,128)(2,1)S(1)}, u32[]{:S(2)}, u32[]{:S(2)}) collective-permute-start(bf16[2,256,256]{1,2,0:T(8,128)(2,1)} %dynamic-slice_convert_fusion.1), channel_id=1, source_target_pairs={{0,1},{1,0},{2,3},{3,2},{4,5},{5,4},{6,7},{7,6},{8,9},{9,8},{10,11... | collective-permute-start | bytes 786440 | tf_op jit(solution)/shard_map/ppermute | solution.py:12
  7.6 0.0 copy-done
  7.7 0.4 fusion.37
  8.0 0.0 slice-done.1
  8.0 1.6 %fusion.9 = f32[2,256,640]{1,2,0:T(8,128)S(1)} fusion(bf16[2048,2,640]{2,1,0:T(2,128)(2,1)S(1)} %slice-done.1, bf16[256,2048]{1,0:T(8,128)(2,1)S(1)} %copy-done.2), kind=kOutput, calls=%fused_computation.19 | convolution fusion | flops 1342177280 | bytes 7602176 | tf_op jit(solution)/shard_map/bf,fek->ebk/dot_general | solution.py:29
  9.7 0.0 copy-start.3
  9.7 0.1 slice.64
  9.7 2.2 %collective-permute-start = (f32[2,256]{1,0:T(2,128)S(1)}, f32[2,256]{1,0:T(2,128)S(1)}, u32[]{:S(2)}, u32[]{:S(2)}) collective-permute-start(f32[2,256]{1,0:T(2,128)S(1)} %fusion.37), channel_id=1, source_target_pairs={{0,1},{1,0},{2,3},{3,2},{4,5},{5,4},{6,7},{7,6},{8,9},{9,8},{10,11... | collective-permute-start | bytes 6152 | tf_op jit(solution)/shard_map/ppermute | solution.py:12
  11.9 0.7 %dynamic-slice_convert_fusion = bf16[2,256,256]{1,2,0:T(8,128)(2,1)} fusion(f32[2,256,512]{1,2,0:T(8,128)S(1)} %slice.64, s32[]{:T(128)S(6)} %select_n.72), kind=kLoop, calls=%fused_computation.29 | loop fusion | bytes 524292 | tf_op jit(solution)/shard_map/convert_element_type | solution.py:35
  12.6 2.6 %collective-permute-start.5 = (bf16[2,256,256]{1,2,0:T(8,128)(2,1)}, bf16[2,256,256]{1,2,0:T(8,128)(2,1)}, u32[]{:S(2)}, u32[]{:S(2)}) collective-permute-start(bf16[2,256,256]{1,2,0:T(8,128)(2,1)} %dynamic-slice_convert_fusion), channel_id=1, source_target_pairs={{0,2},{1,3},{2,0},{3,1},{4,6},{5,7},{6,4},{7,5},{8,10},{9,11},{10,... | collective-permute-start | bytes 786440 | tf_op jit(solution)/shard_map/ppermute | solution.py:12
  15.2 0.0 copy-done.3
  15.3 10.5 %copy.22 = bf16[1024,2,2048]{2,0,1:T(8,128)(2,1)} copy(bf16[1024,2,2048]{2,1,0:T(2,128)(2,1)} %param.7) | data formatting | bytes 16777216 | tf_op args[2]
  25.8 0.0 collective-permute-done
  25.8 0.3 collective-permute-start.1
  26.1 0.0 collective-permute-done.2
  26.1 0.1 fusion.17
  26.2 2.7 %collective-permute-start.3 = (bf16[2,256,256]{1,2,0:T(8,128)(2,1)S(1)}, bf16[2,256,256]{1,2,0:T(8,128)(2,1)S(1)}, u32[]{:S(2)}, u32[]{:S(2)}) collective-permute-start(bf16[2,256,256]{1,2,0:T(8,128)(2,1)S(1)} %fusion.17), channel_id=1, source_target_pairs={{0,2},{1,3},{2,0},{3,1},{4,6},{5,7},{6,4},{7,5},{8,10},{9,11},{10,... | collective-permute-start | bytes 786440 | tf_op jit(solution)/shard_map/ppermute | solution.py:12
  28.8 3.9 %collective-permute-done.1 = f32[2,256]{1,0:T(2,128)S(1)} collective-permute-done((f32[2,256]{1,0:T(2,128)S(1)}, f32[2,256]{1,0:T(2,128)S(1)}, u32[]{:S(2)}, u32[]{:S(2)}) %collective-permute-start.1) | collective-permute-done | bytes 2080 | tf_op jit(solution)/shard_map/ppermute | solution.py:12
  32.8 0.0 collective-permute-done.5
  32.8 1.0 %fusion.18 = bf16[2,256,256]{1,2,0:T(8,128)(2,1)S(1)} fusion(bf16[2,256,256]{1,2,0:T(8,128)(2,1)} %collective-permute-done.5, f32[2,256,512]{1,2,0:T(8,128)S(1)} %slice.64, s32[]{:T(128)S(6)} %select_n.71), kind=kLoop, calls=%fused_computation.34 | loop fusion | flops 393216 | bytes 1048580 | tf_op jit(solution)/shard_map/convert_element_type | solution.py:49
  33.9 0.1 collective-permute-start.6
  33.9 6.0 %collective-permute-done.3 = bf16[2,256,256]{1,2,0:T(8,128)(2,1)S(1)} collective-permute-done((bf16[2,256,256]{1,2,0:T(8,128)(2,1)S(1)}, bf16[2,256,256]{1,2,0:T(8,128)(2,1)S(1)}, u32[]{:S(2)}, u32[]{:S(2)}) %collective-permute-start.3) | collective-permute-done | bytes 262176 | tf_op jit(solution)/shard_map/ppermute | solution.py:12
  40.0 0.0 copy-start.1
  40.0 0.1 tanh_convert_fusion.1
  40.1 0.1 collective-permute-start.4
  40.2 3.7 %collective-permute-done.6 = bf16[2,256,256]{1,2,0:T(8,128)(2,1)S(1)} collective-permute-done((bf16[2,256,256]{1,2,0:T(8,128)(2,1)S(1)}, bf16[2,256,256]{1,2,0:T(8,128)(2,1)S(1)}, u32[]{:S(2)}, u32[]{:S(2)}) %collective-permute-start.6) | collective-permute-done | bytes 262176 | tf_op jit(solution)/shard_map/ppermute | solution.py:12
  43.8 1.1 %tanh_convert_fusion = bf16[2,256,256]{1,2,0:T(8,128)(2,1)S(1)} fusion(bf16[2,256,256]{1,2,0:T(8,128)(2,1)S(1)} %collective-permute-done.6, bf16[2,256,256]{1,2,0:T(8,128)(2,1)} %collective-permute-done.5, f32[2,256,512]{1,2,0:T(8,128)S(1)} %slice.64, s32[]{:T(128)S(6)} %select_n.71), kind=kLoop, calls=%fused_computation.27 | loop fusion | flops 655360 | bytes 1310724 | tf_op jit(solution)/shard_map/convert_element_type | solution.py:50
  44.9 0.1 collective-permute-start.7
  45.0 6.0 %collective-permute-done.4 = bf16[2,256,256]{1,2,0:T(8,128)(2,1)S(1)} collective-permute-done((bf16[2,256,256]{1,2,0:T(8,128)(2,1)S(1)}, bf16[2,256,256]{1,2,0:T(8,128)(2,1)S(1)}, u32[]{:S(2)}, u32[]{:S(2)}) %collective-permute-start.4) | collective-permute-done | bytes 262176 | tf_op jit(solution)/shard_map/ppermute | solution.py:12
  51.0 2.3 %convolution_multiply_fusion.3 = f32[256,2048]{1,0:T(8,128)S(1)} fusion(bf16[2,1024,2048]{2,1,0:T(8,128)(2,1)} %bitcast.42, f32[256]{0:T(256)S(1)} %bitcast.46, bf16[2,256,256]{1,2,0:T(8,128)(2,1)S(1)} %get-tuple-element.12, bf16[2,256,256]{1,2,0:T(8,128)(2,1)S(1)} %get-tuple-element.11), kind=kOutput, calls=%fused_computation.12 | convolution fusion | flops 537919488 | bytes 4719616 | tf_op jit(solution)/shard_map/dot_general | solution.py:58
  53.4 0.0 copy-done.1
  53.4 0.7 %fusion.6 = f32[256,2048]{1,0:T(8,128)S(1)} fusion(f32[256,2048]{1,0:T(8,128)S(1)} %convolution_multiply_fusion.3, bf16[2,1024,2048]{2,1,0:T(8,128)(2,1)S(1)} %bitcast.43, f32[256]{0:T(256)S(1)} %bitcast.51, bf16[2,256,256]{1,2,0:T(8,128)(2,1)S(1)} %get-tuple-element.11, bf16[2,256,256]{1,2,0:T(8,128)(2,1)S(1)} %get-tuple-element.12), kind=kOutput, calls=%fused_computation.11 | convolution fusion | flops 538443776 | bytes 6816768 | tf_op jit(solution)/shard_map/dot_general | solution.py:58
  54.1 3.3 %collective-permute-done.7 = bf16[2,256,256]{1,2,0:T(8,128)(2,1)S(1)} collective-permute-done((bf16[2,256,256]{1,2,0:T(8,128)(2,1)S(1)}, bf16[2,256,256]{1,2,0:T(8,128)(2,1)S(1)}, u32[]{:S(2)}, u32[]{:S(2)}) %collective-permute-start.7) | collective-permute-done | bytes 262176 | tf_op jit(solution)/shard_map/ppermute | solution.py:12
  57.5 0.7 %fusion.5 = f32[256,2048]{1,0:T(8,128)S(1)} fusion(f32[256,2048]{1,0:T(8,128)S(1)} %fusion.6, bf16[2,1024,2048]{2,1,0:T(8,128)(2,1)S(1)} %bitcast.44, f32[256]{0:T(256)S(1)} %bitcast.47, bf16[2,256,256]{1,2,0:T(8,128)(2,1)S(1)} %get-tuple-element.10, bf16[2,256,256]{1,2,0:T(8,128)(2,1)S(1)} %get-tuple-element.9), kind=kOutput, calls=%fused_computation.9 | convolution fusion | flops 538443776 | bytes 6816768 | tf_op jit(solution)/shard_map/dot_general | solution.py:58
  58.2 2.1 %fusion.8 = bf16[256,2048]{1,0:T(8,128)(2,1)} fusion(f32[256,2048]{1,0:T(8,128)S(1)} %fusion.5, bf16[2,1024,2048]{2,1,0:T(8,128)(2,1)S(1)} %bitcast.45, bf16[256,2048]{1,0:T(8,128)(2,1)S(1)} %copy-done.2, f32[2048]{0:T(1024)S(1)} %bitcast.50, f32[2048]{0:T(1024)S(1)} %bitcast.49, f32[256]{0:T(256)S(1)} %bitcast.52, f32[256]{0:T(256)S(1)} %bitcast.48, ...), kind=kOutput, calls=%fused_computation.14 | convolution fusion | flops 542638080 | bytes 6834176 | tf_op jit(solution)/shard_map/dot_general | solution.py:58
  (6 shorter events, 0.1 us)
Async XLA Ops:
  0.0 7.7 %copy-start = (bf16[2048,2]{0,1:T(2,128)(2,1)S(1)}, bf16[2048,2]{0,1:T(2,128)(2,1)}, u32[]{:S(2)}) copy-start(bf16[2048,2]{0,1:T(2,128)(2,1)} %param.8) | copy-start | bytes 24580
  0.0 2.5 %slice-start = ((bf16[2048,2,1024]{2,1,0:T(2,128)(2,1)}), bf16[2048,2,512]{2,1,0:T(2,128)(2,1)S(1)}, s32[]{:S(2)}) async-start(bf16[2048,2,1024]{2,1,0:T(2,128)(2,1)} %param.6), calls=%async_computation | async-start | bytes 8388608 | tf_op jit(solution)/shard_map/slice | solution.py:30
  0.0 2.5 %copy-start.2 = (bf16[256,2048]{1,0:T(8,128)(2,1)S(1)}, bf16[256,2048]{1,0:T(8,128)(2,1)}, u32[]{:S(2)}) copy-start(bf16[256,2048]{1,0:T(8,128)(2,1)} %param.5) | copy-start | bytes 3145732
  4.6 3.4 %slice-start.1 = ((bf16[2048,2,1024]{2,1,0:T(2,128)(2,1)}), bf16[2048,2,640]{2,1,0:T(2,128)(2,1)S(1)}, s32[]{:S(2)}) async-start(bf16[2048,2,1024]{2,1,0:T(2,128)(2,1)} %param.6), calls=%async_computation.1 | async-start | bytes 10485760 | tf_op jit(solution)/shard_map/slice | solution.py:30
  4.6 21.5 %collective-permute-start.2 = (bf16[2,256,256]{1,2,0:T(8,128)(2,1)}, bf16[2,256,256]{1,2,0:T(8,128)(2,1)S(1)}, u32[]{:S(2)}, u32[]{:S(2)}) collective-permute-start(bf16[2,256,256]{1,2,0:T(8,128)(2,1)} %dynamic-slice_convert_fusion.1), channel_id=1, source_target_pairs={{0,1},{1,0},{2,3},{3,2},{4,5},{5,4},{6,7},{7,6},{8,9},{9,8},{10,11... | collective-permute-start | bytes 786440 | tf_op jit(solution)/shard_map/ppermute | solution.py:12
  9.7 5.6 %copy-start.3 = (f32[2,2048]{1,0:T(2,128)S(1)}, f32[2,2048]{1,0:T(2,128)}, u32[]{:S(2)}) copy-start(f32[2,2048]{1,0:T(2,128)} %param.9) | copy-start | bytes 49156
  9.7 16.0 %collective-permute-start = (f32[2,256]{1,0:T(2,128)S(1)}, f32[2,256]{1,0:T(2,128)S(1)}, u32[]{:S(2)}, u32[]{:S(2)}) collective-permute-start(f32[2,256]{1,0:T(2,128)S(1)} %fusion.37), channel_id=1, source_target_pairs={{0,1},{1,0},{2,3},{3,2},{4,5},{5,4},{6,7},{7,6},{8,9},{9,8},{10,11... | collective-permute-start | bytes 6152 | tf_op jit(solution)/shard_map/ppermute | solution.py:12
  12.6 20.2 %collective-permute-start.5 = (bf16[2,256,256]{1,2,0:T(8,128)(2,1)}, bf16[2,256,256]{1,2,0:T(8,128)(2,1)}, u32[]{:S(2)}, u32[]{:S(2)}) collective-permute-start(bf16[2,256,256]{1,2,0:T(8,128)(2,1)} %dynamic-slice_convert_fusion), channel_id=1, source_target_pairs={{0,2},{1,3},{2,0},{3,1},{4,6},{5,7},{6,4},{7,5},{8,10},{9,11},{10,... | collective-permute-start | bytes 786440 | tf_op jit(solution)/shard_map/ppermute | solution.py:12
  25.8 7.0 %collective-permute-start.1 = (f32[2,256]{1,0:T(2,128)S(1)}, f32[2,256]{1,0:T(2,128)S(1)}, u32[]{:S(2)}, u32[]{:S(2)}) collective-permute-start(f32[2,256]{1,0:T(2,128)S(1)} %add.64), channel_id=1, source_target_pairs={{0,2},{1,3},{2,0},{3,1},{4,6},{5,7},{6,4},{7,5},{8,10},{9,11},{10,... | collective-permute-start | bytes 6152 | tf_op jit(solution)/shard_map/ppermute | solution.py:12
  26.2 13.8 %collective-permute-start.3 = (bf16[2,256,256]{1,2,0:T(8,128)(2,1)S(1)}, bf16[2,256,256]{1,2,0:T(8,128)(2,1)S(1)}, u32[]{:S(2)}, u32[]{:S(2)}) collective-permute-start(bf16[2,256,256]{1,2,0:T(8,128)(2,1)S(1)} %fusion.17), channel_id=1, source_target_pairs={{0,2},{1,3},{2,0},{3,1},{4,6},{5,7},{6,4},{7,5},{8,10},{9,11},{10,... | collective-permute-start | bytes 786440 | tf_op jit(solution)/shard_map/ppermute | solution.py:12
  33.9 10.0 %collective-permute-start.6 = (bf16[2,256,256]{1,2,0:T(8,128)(2,1)S(1)}, bf16[2,256,256]{1,2,0:T(8,128)(2,1)S(1)}, u32[]{:S(2)}, u32[]{:S(2)}) collective-permute-start(bf16[2,256,256]{1,2,0:T(8,128)(2,1)S(1)} %fusion.18), channel_id=1, source_target_pairs={{0,1},{1,0},{2,3},{3,2},{4,5},{5,4},{6,7},{7,6},{8,9},{9,8},{10,11... | collective-permute-start | bytes 786440 | tf_op jit(solution)/shard_map/ppermute | solution.py:12
  40.0 13.4 %copy-start.1 = (bf16[1024,2,2048]{2,0,1:T(8,128)(2,1)S(1)}, bf16[1024,2,2048]{2,0,1:T(8,128)(2,1)}, u32[]{:S(2)}) copy-start(bf16[1024,2,2048]{2,0,1:T(8,128)(2,1)} %copy.22) | copy-start | bytes 25165828
  40.1 10.9 %collective-permute-start.4 = (bf16[2,256,256]{1,2,0:T(8,128)(2,1)S(1)}, bf16[2,256,256]{1,2,0:T(8,128)(2,1)S(1)}, u32[]{:S(2)}, u32[]{:S(2)}) collective-permute-start(bf16[2,256,256]{1,2,0:T(8,128)(2,1)S(1)} %tanh_convert_fusion.1), channel_id=1, source_target_pairs={{0,1},{1,0},{2,3},{3,2},{4,5},{5,4},{6,7},{7,6},{8,9},{9,8},{10,11... | collective-permute-start | bytes 786440 | tf_op jit(solution)/shard_map/ppermute | solution.py:12
  44.9 12.5 %collective-permute-start.7 = (bf16[2,256,256]{1,2,0:T(8,128)(2,1)S(1)}, bf16[2,256,256]{1,2,0:T(8,128)(2,1)S(1)}, u32[]{:S(2)}, u32[]{:S(2)}) collective-permute-start(bf16[2,256,256]{1,2,0:T(8,128)(2,1)S(1)} %tanh_convert_fusion), channel_id=1, source_target_pairs={{0,2},{1,3},{2,0},{3,1},{4,6},{5,7},{6,4},{7,5},{8,10},{9,11},{10,... | collective-permute-start | bytes 786440 | tf_op jit(solution)/shard_map/ppermute | solution.py:12

commit v4 on v3

v4 whole, which is shorter than its diff:
```python
import jax
import jax.numpy as jnp
from jax import lax
from jax.experimental import pallas as pl
from jax.experimental.pallas import tpu as pltpu
from jax.sharding import PartitionSpec as P


LANES = 128
BF16 = jnp.bfloat16
F32 = jnp.float32


def swap(value, bit, size):
    return lax.ppermute(value, "width", [(i, i ^ bit) for i in range(size)])


def turn_kernel(stored_ref, after_ref, out_ref):
    depth, experts, columns = stored_ref.shape
    row = lax.broadcasted_iota(jnp.int32, (experts * depth, experts * depth), 0)
    lane = lax.broadcasted_iota(jnp.int32, (experts * depth, experts * depth), 1)
    ones = (lane == row % depth * experts + row // depth).astype(BF16)
    block = stored_ref[...].reshape(depth * experts, columns)
    turned = jnp.dot(ones, block, preferred_element_type=F32).astype(BF16)
    for e in range(experts):
        out_ref[e] = turned[e * depth : (e + 1) * depth]


def turn(rank_up, start, size, after):
    _, experts, columns = rank_up.shape
    depth = LANES
    return pl.pallas_call(
        turn_kernel,
        grid=(size // depth,),
        in_specs=[
            pl.BlockSpec((depth, experts, columns), lambda i: (start // depth + i, 0, 0)),
            pl.BlockSpec(memory_space=pl.ANY),
        ],
        out_specs=pl.BlockSpec((experts, depth, columns), lambda i: (0, i, 0)),
        out_shape=jax.ShapeDtypeStruct((experts, size, columns), rank_up.dtype),
        compiler_params=pltpu.CompilerParams(vmem_limit_bytes=16 << 20),
        cost_estimate=pl.CostEstimate(
            flops=4 * size * experts * experts * depth * columns,
            bytes_accessed=4 * size * experts * columns,
            transcendentals=0,
        ),
    )(rank_up, after)


def half(value, which):
    n = value.shape[-1] // 2
    return lax.dynamic_slice_in_dim(value, which * n, n, axis=value.ndim - 1)


def layer(samples, rank_down, rank_up, gate_proj, expert_bias):
    size = lax.axis_size("width")
    me = lax.axis_index("width")
    experts, rank = rank_down.shape[1:]
    bits = [1 << i for i in range(size.bit_length() - 1)]
    orders = [bits, bits[::-1]]
    cut = rank // 2

    held = [jnp.einsum("bf,fek->ebk", samples, rank_down[:, :, :cut], preferred_element_type=F32)]
    again, held[0] = lax.optimization_barrier((samples, held[0]))
    wide = jnp.einsum("bf,fek->ebk", again, rank_down[:, :, cut - LANES :], preferred_element_type=F32)
    logits = jnp.transpose(jnp.dot(again, gate_proj, preferred_element_type=F32))
    logits, wide = lax.optimization_barrier((logits, wide[:, :, -cut:]))
    held.append(wide)
    sent = [half(held[s], 1 - me // orders[s][0] % 2).astype(BF16) for s in range(2)]
    arrived = [swap(sent[s], orders[s][0], size) for s in range(2)]
    for bit in bits:
        logits = logits + swap(logits, bit, size)
    gate = jax.nn.sigmoid(logits)

    totals = []
    for s, order in enumerate(orders):
        total = half(held[s], me // order[0] % 2) + arrived[s].astype(F32)
        for bit in order[1:-1]:
            mine = me // bit % 2
            part = swap(half(total, 1 - mine).astype(BF16), bit, size)
            total = half(total, mine) + part.astype(F32)
        totals.append((total, total.astype(BF16)))
    up = [turn(rank_up, s * cut, cut, after) for s, after in enumerate((sent[1], totals[1][1]))]
    terms = []
    for s, order in enumerate(orders):
        total, message = totals[s]
        total = total + swap(message, order[-1], size).astype(F32)
        have = jnp.tanh(total).astype(BF16)
        for bit in order[:-1][::-1]:
            part = swap(have, bit, size)
            low = me // bit % 2 == 0
            have = jnp.concatenate([jnp.where(low, have, part), jnp.where(low, part, have)], axis=2)
        for e in range(experts):
            terms.append(
                gate[e][:, None]
                * jnp.dot(have[e], up[s][e], preferred_element_type=F32)
            )
    bias = sum(gate[e][:, None] * expert_bias[e][None] for e in range(experts))
    blended = sum(terms, bias)
    inputs = samples.astype(F32)
    return (inputs * blended + inputs).astype(BF16)


def solution(mesh):
    placed = (
        P("batch", "width"),
        P("width", None, None),
        P(None, None, "width"),
        P("width", None),
        P(None, "width"),
    )
    return jax.shard_map(
        layer, mesh=mesh, in_specs=placed, out_specs=P("batch", "width"), check_vma=False
    )
```

time: 60.6 us -> 64.3 us (1.061)
  Pallas kernels: 0 us -> 4.17 us
  starting transfers between devices: 11 us -> 15 us
  waiting for transfers between devices: 22.9 us -> 19.9 us
  other arithmetic: 2.39 us -> 4.34 us
  matrix products: 9.24 us -> 7.47 us
  local copies, waits for them, and re-layouts: 14.6 us -> 12.9 us
    pallas_call x0 -> x2, Pallas kernels: none -> 4.17 us  [turn(): pl.pallas_call(turn_kernel, grid=(size // depth,), in_specs=[pl.BlockSpec...]
    ppermute x8, starting transfers between devices: 11 us -> 15 us  [swap(): return lax.ppermute(value, 'width', [(i, i ^ bit) for i in range(size)])]
    ppermute x8, waiting for transfers between devices: 22.9 us -> 19.9 us  [swap(): return lax.ppermute(value, 'width', [(i, i ^ bit) for i in range(size)])]
    convert_element_type x4, other arithmetic: 2.3 us -> 4.24 us  [the longest x2 2.17 us: layer(): have = jnp.tanh(total).astype(BF16)]
    unnamed x9 -> x14, local copies, waits for them, and re-layouts: 10.5 us -> 8.71 us
    dot_general x7, matrix products: 9.24 us -> 7.47 us  [the longest x4 4.23 us: layer(): jnp.dot(have[e], up[s][e], preferred_element_type=F32)]
    slice x7, local copies, waits for them, and re-layouts: 2.61 us -> 3.43 us  [the longest x2 2.51 us: layer(): rank_down[:, :, :cut]]
    convert_element_type x2, local copies, waits for them, and re-layouts: 1.47 us -> 0.76 us  [layer(): half(held[s], 1 - me // orders[s][0] % 2).astype(BF16)]
  transfers between devices with their start and end apart: 8 -> 8, of which waited for: 5 -> 4; matrix products, arithmetic and copies ran while one was open for 31% -> 10% of each run, Pallas kernels for 0% -> 7%
where the time goes in v4:
time: 64.3 us; the launch traced here: 64 us
  waiting for transfers between devices  19.9 us (31%)
  starting transfers between devices  15 us (23%)
  local copies, waits for them, and re-layouts  12.9 us (20%)
  matrix products  7.47 us (12%)
  other arithmetic  4.34 us (7%)
  Pallas kernels  4.17 us (6%)
    ppermute x8, waiting for transfers between devices, swap(): return lax.ppermute(value, 'width', [(i, i ^ bit) for i in range(size)])  19.9 us
    ppermute x8, starting transfers between devices, swap(): return lax.ppermute(value, 'width', [(i, i ^ bit) for i in range(size)])  15 us
    unnamed x14, local copies, waits for them, and re-layouts  8.71 us
    dot_general x4, matrix products, layer(): jnp.dot(have[e], up[s][e], preferred_element_type=F32)  4.23 us
    pallas_call x2, Pallas kernels, turn(): pl.pallas_call(turn_kernel, grid=(size // depth,), in_specs=[pl.BlockSpec...  4.17 us
    slice x2, local copies, waits for them, and re-layouts, layer(): rank_down[:, :, :cut]  2.51 us
    convert_element_type x2, other arithmetic, layer(): have = jnp.tanh(total).astype(BF16)  2.17 us
    convert_element_type x2, other arithmetic, layer(): totals.append((total, total.astype(BF16)))  2.07 us
  transfers between devices with their start and end apart: 8, of which 4 were waited for; matrix products, arithmetic and copies ran while one was open for 10% of the time, Pallas kernels for 7%

profile of v4, /device:TPU:0, one launch (start us, length us, event | category | flops | bytes accessed | tf_op | source)
XLA Modules:
  0.0 64.0 jit_solution(11734244124108368796)
XLA Ops:
  0.0 0.0 copy-start
  0.0 0.0 slice-start
  0.0 0.0 copy-start.5
  0.0 2.5 %slice-done = bf16[2048,2,512]{2,1,0:T(2,128)(2,1)S(1)} async-done(((bf16[2048,2,1024]{2,1,0:T(2,128)(2,1)}), bf16[2048,2,512]{2,1,0:T(2,128)(2,1)S(1)}, s32[]{:S(2)}) %slice-start) | async-done | bytes 4194328 | tf_op jit(solution)/shard_map/slice | solution.py:63
  2.5 0.0 copy-done.5
  2.5 0.0 slice-start.1
  2.5 1.3 %fusion.12 = f32[2,256,512]{1,2,0:T(8,128)S(1)} fusion(bf16[2048,2,512]{2,1,0:T(2,128)(2,1)S(1)} %slice-done, bf16[256,2048]{1,0:T(8,128)(2,1)S(1)} %copy-done.5), kind=kOutput, calls=%fused_computation.19 | convolution fusion | flops 1073741824 | bytes 6291456 | tf_op jit(solution)/shard_map/bf,fek->ebk/dot_general | solution.py:63
  3.9 0.0 copy-done
  3.9 0.4 convolution_bitcast_fusion
  4.2 0.8 %slice-done.1 = bf16[2048,2,640]{2,1,0:T(2,128)(2,1)S(1)} async-done(((bf16[2048,2,1024]{2,1,0:T(2,128)(2,1)}), bf16[2048,2,640]{2,1,0:T(2,128)(2,1)S(1)}, s32[]{:S(2)}) %slice-start.1) | async-done | bytes 5242904 | tf_op jit(solution)/shard_map/slice | solution.py:65
  5.0 1.5 %fusion.9 = f32[2,256,640]{2,1,0:T(8,128)S(1)} fusion(bf16[2048,2,640]{2,1,0:T(2,128)(2,1)S(1)} %slice-done.1, bf16[256,2048]{1,0:T(8,128)(2,1)S(1)} %copy-done.5), kind=kOutput, calls=%fused_computation.18 | convolution fusion | flops 1342177280 | bytes 7602176 | tf_op jit(solution)/shard_map/bf,fek->ebk/dot_general | solution.py:65
  6.6 0.0 copy-start.6
  6.6 0.1 slice.64
  6.7 3.1 %collective-permute-start = (f32[2,256]{1,0:T(2,128)S(1)}, f32[2,256]{1,0:T(2,128)S(1)}, u32[]{:S(2)}, u32[]{:S(2)}) collective-permute-start(f32[2,256]{1,0:T(2,128)S(1)} %convolution_bitcast_fusion), channel_id=1, source_target_pairs={{0,1},{1,0},{2,3},{3,2},{4,5},{5,4},{6,7},{7,6},{8,9},{9,8},{10,11... | collective-permute-start | bytes 6152 | tf_op jit(solution)/shard_map/ppermute | solution.py:15
  9.8 0.7 %dynamic-slice_convert_fusion.1 = bf16[2,256,256]{1,2,0:T(8,128)(2,1)} fusion(f32[2,256,512]{1,2,0:T(8,128)S(1)} %fusion.12, s32[]{:T(128)S(6)} %select_n.65), kind=kLoop, calls=%fused_computation.32 | loop fusion | bytes 524292 | tf_op jit(solution)/shard_map/convert_element_type | solution.py:69
  10.5 0.0 collective-permute-start.2
  10.6 3.1 %collective-permute-start.5 = (bf16[2,256,256]{2,1,0:T(8,128)(2,1)S(1)}, bf16[2,256,256]{2,1,0:T(8,128)(2,1)}, u32[]{:S(2)}, u32[]{:S(2)}) collective-permute-start(bf16[2,256,256]{2,1,0:T(8,128)(2,1)S(1)} %dynamic-slice_convert_fusion.after_ref), channel_id=1, source_target_pairs={{0,2},{1,3},{2,0},{3,1},{4,6},{5,7},{6,4},{7,5},{8,10},{9,11},{10,... | collective-permute-start | bytes 786440 | tf_op jit(solution)/shard_map/ppermute | solution.py:15
  13.7 0.0 copy-done.6
  13.7 0.0 collective-permute-done
  13.7 0.7 %collective-permute-start.1 = (f32[2,256]{1,0:T(2,128)S(1)}, f32[2,256]{1,0:T(2,128)S(1)}, u32[]{:S(2)}, u32[]{:S(2)}) collective-permute-start(f32[2,256]{1,0:T(2,128)S(1)} %add.64), channel_id=1, source_target_pairs={{0,2},{1,3},{2,0},{3,1},{4,6},{5,7},{6,4},{7,5},{8,10},{9,11},{10,... | collective-permute-start | bytes 6152 | tf_op jit(solution)/shard_map/ppermute | solution.py:15
  14.4 0.0 copy-start.1
  14.4 3.4 %copy-done.1 = bf16[1024,2,2048]{2,1,0:T(2,128)(2,1)S(1)} copy-done((bf16[1024,2,2048]{2,1,0:T(2,128)(2,1)S(1)}, bf16[1024,2,2048]{2,1,0:T(2,128)(2,1)}, u32[]{:S(2)}) %copy-start.1) | copy-done | bytes 8388632
  17.8 2.1 %shard_map.55 = bf16[2,512,2048]{2,1,0:T(8,128)(2,1)S(1)} custom-call(bf16[1024,2,2048]{2,1,0:T(2,128)(2,1)S(1)} %copy-done.1, bf16[2,256,256]{2,1,0:T(8,128)(2,1)S(1)} %dynamic-slice_convert_fusion.after_ref), custom_call_target="tpu_custom_call" | custom-call | flops 2147483648 | bytes 8388608 | tf_op jit(solution)/shard_map/pallas_call | solution.py:32
  19.9 0.0 copy-start.3
  19.9 1.9 %copy-done.3 = bf16[2,512,2048]{2,1,0:T(8,128)(2,1)} copy-done((bf16[2,512,2048]{2,1,0:T(8,128)(2,1)}, bf16[2,512,2048]{2,1,0:T(8,128)(2,1)S(1)}, u32[]{:S(2)}) %copy-start.3) | copy-done | bytes 4194328
  21.8 0.2 collective-permute-done.1
  22.1 2.2 %collective-permute-done.2 = bf16[2,256,256]{1,2,0:T(8,128)(2,1)} collective-permute-done((bf16[2,256,256]{1,2,0:T(8,128)(2,1)}, bf16[2,256,256]{1,2,0:T(8,128)(2,1)}, u32[]{:S(2)}, u32[]{:S(2)}) %collective-permute-start.2) | collective-permute-done | bytes 262176 | tf_op jit(solution)/shard_map/ppermute | solution.py:15
  24.3 1.0 %fusion.17 = bf16[2,256,256]{1,2,0:T(8,128)(2,1)S(1)} fusion(bf16[2,256,256]{1,2,0:T(8,128)(2,1)} %collective-permute-done.2, f32[2,256,512]{1,2,0:T(8,128)S(1)} %fusion.12, s32[]{:T(128)S(6)} %select_n.64), kind=kLoop, calls=%fused_computation.33 | loop fusion | flops 393216 | bytes 1048580 | tf_op jit(solution)/shard_map/convert_element_type | solution.py:82
  25.3 1.4 %collective-permute-start.3 = (bf16[2,256,256]{1,2,0:T(8,128)(2,1)S(1)}, bf16[2,256,256]{1,2,0:T(8,128)(2,1)S(1)}, u32[]{:S(2)}, u32[]{:S(2)}) collective-permute-start(bf16[2,256,256]{1,2,0:T(8,128)(2,1)S(1)} %fusion.17), channel_id=1, source_target_pairs={{0,2},{1,3},{2,0},{3,1},{4,6},{5,7},{6,4},{7,5},{8,10},{9,11},{10,... | collective-permute-start | bytes 786440 | tf_op jit(solution)/shard_map/ppermute | solution.py:15
  26.7 0.0 collective-permute-done.5
  26.7 1.1 %fusion.18.after_ref = bf16[2,256,256]{2,1,0:T(8,128)(2,1)S(1)} fusion(bf16[2,256,256]{2,1,0:T(8,128)(2,1)} %collective-permute-done.5, f32[2,256,512]{2,1,0:T(8,128)S(1)} %slice.64, s32[]{:T(128)S(6)} %select_n.72), kind=kLoop, calls=%fused_computation.34 | loop fusion | flops 393216 | bytes 1048580 | tf_op jit(solution)/shard_map/convert_element_type | solution.py:82
  27.8 3.9 %collective-permute-start.6 = (bf16[2,256,256]{2,1,0:T(8,128)(2,1)S(1)}, bf16[2,256,256]{2,1,0:T(8,128)(2,1)S(1)}, u32[]{:S(2)}, u32[]{:S(2)}) collective-permute-start(bf16[2,256,256]{2,1,0:T(8,128)(2,1)S(1)} %fusion.18.after_ref), channel_id=1, source_target_pairs={{0,1},{1,0},{2,3},{3,2},{4,5},{5,4},{6,7},{7,6},{8,9},{9,8},{10,11... | collective-permute-start | bytes 786440 | tf_op jit(solution)/shard_map/ppermute | solution.py:15
  31.7 7.6 %collective-permute-done.3 = bf16[2,256,256]{1,2,0:T(8,128)(2,1)S(1)} collective-permute-done((bf16[2,256,256]{1,2,0:T(8,128)(2,1)S(1)}, bf16[2,256,256]{1,2,0:T(8,128)(2,1)S(1)}, u32[]{:S(2)}, u32[]{:S(2)}) %collective-permute-start.3) | collective-permute-done | bytes 262176 | tf_op jit(solution)/shard_map/ppermute | solution.py:15
  39.3 1.1 %tanh_convert_fusion.1 = bf16[2,256,256]{1,2,0:T(8,128)(2,1)S(1)} fusion(bf16[2,256,256]{1,2,0:T(8,128)(2,1)S(1)} %collective-permute-done.3, bf16[2,256,256]{1,2,0:T(8,128)(2,1)} %collective-permute-done.2, f32[2,256,512]{1,2,0:T(8,128)S(1)} %fusion.12, s32[]{:T(128)S(6)} %select_n.64), kind=kLoop, calls=%fused_computation.30 | loop fusion | flops 655360 | bytes 1310724 | tf_op jit(solution)/shard_map/convert_element_type | solution.py:88
  40.4 0.1 collective-permute-start.4
  40.5 0.0 copy-start.2
  40.5 3.4 %copy-done.2 = bf16[1024,2,2048]{2,1,0:T(2,128)(2,1)S(1)} copy-done((bf16[1024,2,2048]{2,1,0:T(2,128)(2,1)S(1)}, bf16[1024,2,2048]{2,1,0:T(2,128)(2,1)}, u32[]{:S(2)}) %copy-start.2) | copy-done | bytes 8388632
  43.9 2.1 %shard_map.56 = bf16[2,512,2048]{2,1,0:T(8,128)(2,1)S(1)} custom-call(bf16[1024,2,2048]{2,1,0:T(2,128)(2,1)S(1)} %copy-done.2, bf16[2,256,256]{2,1,0:T(8,128)(2,1)S(1)} %fusion.18.after_ref), custom_call_target="tpu_custom_call" | custom-call | flops 2147483648 | bytes 8388608 | tf_op jit(solution)/shard_map/pallas_call | solution.py:32
  46.0 0.0 collective-permute-done.6
  46.0 1.1 %tanh_convert_fusion = bf16[2,256,256]{2,1,0:T(8,128)(2,1)S(1)} fusion(bf16[2,256,256]{2,1,0:T(8,128)(2,1)S(1)} %collective-permute-done.6, bf16[2,256,256]{2,1,0:T(8,128)(2,1)} %collective-permute-done.5, f32[2,256,512]{2,1,0:T(8,128)S(1)} %slice.64, s32[]{:T(128)S(6)} %select_n.72), kind=kLoop, calls=%fused_computation.27 | loop fusion | flops 655360 | bytes 1310724 | tf_op jit(solution)/shard_map/convert_element_type | solution.py:88
  47.1 2.7 %collective-permute-start.7 = (bf16[2,256,256]{2,1,0:T(8,128)(2,1)S(1)}, bf16[2,256,256]{2,1,0:T(8,128)(2,1)S(1)}, u32[]{:S(2)}, u32[]{:S(2)}) collective-permute-start(bf16[2,256,256]{2,1,0:T(8,128)(2,1)S(1)} %tanh_convert_fusion), channel_id=1, source_target_pairs={{0,2},{1,3},{2,0},{3,1},{4,6},{5,7},{6,4},{7,5},{8,10},{9,11},{10,... | collective-permute-start | bytes 786440 | tf_op jit(solution)/shard_map/ppermute | solution.py:15
  49.8 0.0 collective-permute-done.4
  49.8 0.0 copy-done.4
  49.8 0.8 %fusion.7 = f32[256,2048]{1,0:T(8,128)S(1)} fusion(bf16[2,512,2048]{2,1,0:T(8,128)(2,1)S(1)} %copy-done.4, f32[2048]{0:T(1024)S(1)} %bitcast.46, f32[256]{0:T(256)S(1)} %bitcast.42, f32[2048]{0:T(1024)S(1)} %bitcast.45, f32[256]{0:T(256)S(1)} %bitcast.47, bf16[2,256,256]{1,2,0:T(8,128)(2,1)S(1)} %get-tuple-element.16, ...), kind=kOutput, calls=%fused_computation.12 | convolution fusion | flops 540016640 | bytes 4737024 | tf_op jit(solution)/shard_map/dot_general | solution.py:96
  50.7 0.7 %fusion.6 = f32[256,2048]{1,0:T(8,128)S(1)} fusion(f32[256,2048]{1,0:T(8,128)S(1)} %fusion.7, bf16[2,512,2048]{2,1,0:T(8,128)(2,1)S(1)} %copy-done.4, f32[256]{0:T(256)S(1)} %bitcast.43, bf16[2,256,256]{1,2,0:T(8,128)(2,1)S(1)} %get-tuple-element.15, bf16[2,256,256]{1,2,0:T(8,128)(2,1)S(1)} %get-tuple-element.16), kind=kOutput, calls=%fused_computation.10 | convolution fusion | flops 538443776 | bytes 6816768 | tf_op jit(solution)/shard_map/dot_general | solution.py:96
  51.4 9.9 %collective-permute-done.7 = bf16[2,256,256]{2,1,0:T(8,128)(2,1)S(1)} collective-permute-done((bf16[2,256,256]{2,1,0:T(8,128)(2,1)S(1)}, bf16[2,256,256]{2,1,0:T(8,128)(2,1)S(1)}, u32[]{:S(2)}, u32[]{:S(2)}) %collective-permute-start.7) | collective-permute-done | bytes 262176 | tf_op jit(solution)/shard_map/ppermute | solution.py:15
  61.3 0.8 %fusion.5 = f32[256,2048]{1,0:T(8,128)S(1)} fusion(f32[256,2048]{1,0:T(8,128)S(1)} %fusion.6, bf16[2,512,2048]{2,1,0:T(8,128)(2,1)S(1)} %shard_map.56, f32[256]{0:T(256)S(1)} %bitcast.48, bf16[2,256,256]{2,1,0:T(8,128)(2,1)S(1)} %get-tuple-element.14, bf16[2,256,256]{2,1,0:T(8,128)(2,1)S(1)} %get-tuple-element.13), kind=kOutput, calls=%fused_computation.8 | convolution fusion | flops 538443776 | bytes 6816768 | tf_op jit(solution)/shard_map/dot_general | solution.py:96
  62.1 1.9 %fusion.8 = bf16[256,2048]{1,0:T(8,128)(2,1)} fusion(f32[256,2048]{1,0:T(8,128)S(1)} %fusion.5, bf16[2,512,2048]{2,1,0:T(8,128)(2,1)S(1)} %shard_map.56, bf16[256,2048]{1,0:T(8,128)(2,1)S(1)} %copy-done.5, f32[256]{0:T(256)S(1)} %bitcast.44, bf16[2,256,256]{2,1,0:T(8,128)(2,1)S(1)} %get-tuple-element.13, bf16[2,256,256]{2,1,0:T(8,128)(2,1)S(1)} %get-tuple-element.14), kind=kOutput, calls=%fused_computation.13 | convolution fusion | flops 540540928 | bytes 6816768 | tf_op jit(solution)/shard_map/dot_general | solution.py:96
  (8 shorter events, 0.1 us)
Async XLA Ops:
  0.0 3.9 %copy-start = (bf16[2048,2]{0,1:T(2,128)(2,1)S(1)}, bf16[2048,2]{0,1:T(2,128)(2,1)}, u32[]{:S(2)}) copy-start(bf16[2048,2]{0,1:T(2,128)(2,1)} %param.8) | copy-start | bytes 24580
  0.0 2.5 %slice-start = ((bf16[2048,2,1024]{2,1,0:T(2,128)(2,1)}), bf16[2048,2,512]{2,1,0:T(2,128)(2,1)S(1)}, s32[]{:S(2)}) async-start(bf16[2048,2,1024]{2,1,0:T(2,128)(2,1)} %param.6), calls=%async_computation | async-start | bytes 8388608 | tf_op jit(solution)/shard_map/slice | solution.py:63
  0.0 2.5 %copy-start.5 = (bf16[256,2048]{1,0:T(8,128)(2,1)S(1)}, bf16[256,2048]{1,0:T(8,128)(2,1)}, u32[]{:S(2)}) copy-start(bf16[256,2048]{1,0:T(8,128)(2,1)} %param.5) | copy-start | bytes 3145732
  2.5 2.5 %slice-start.1 = ((bf16[2048,2,1024]{2,1,0:T(2,128)(2,1)}), bf16[2048,2,640]{2,1,0:T(2,128)(2,1)S(1)}, s32[]{:S(2)}) async-start(bf16[2048,2,1024]{2,1,0:T(2,128)(2,1)} %param.6), calls=%async_computation.1 | async-start | bytes 10485760 | tf_op jit(solution)/shard_map/slice | solution.py:65
  6.6 7.1 %copy-start.6 = (f32[2,2048]{1,0:T(2,128)S(1)}, f32[2,2048]{1,0:T(2,128)}, u32[]{:S(2)}) copy-start(f32[2,2048]{1,0:T(2,128)} %param.9) | copy-start | bytes 49156
  6.7 7.0 %collective-permute-start = (f32[2,256]{1,0:T(2,128)S(1)}, f32[2,256]{1,0:T(2,128)S(1)}, u32[]{:S(2)}, u32[]{:S(2)}) collective-permute-start(f32[2,256]{1,0:T(2,128)S(1)} %convolution_bitcast_fusion), channel_id=1, source_target_pairs={{0,1},{1,0},{2,3},{3,2},{4,5},{5,4},{6,7},{7,6},{8,9},{9,8},{10,11... | collective-permute-start | bytes 6152 | tf_op jit(solution)/shard_map/ppermute | solution.py:15
  10.5 13.7 %collective-permute-start.2 = (bf16[2,256,256]{1,2,0:T(8,128)(2,1)}, bf16[2,256,256]{1,2,0:T(8,128)(2,1)}, u32[]{:S(2)}, u32[]{:S(2)}) collective-permute-start(bf16[2,256,256]{1,2,0:T(8,128)(2,1)} %dynamic-slice_convert_fusion.1), channel_id=1, source_target_pairs={{0,1},{1,0},{2,3},{3,2},{4,5},{5,4},{6,7},{7,6},{8,9},{9,8},{10,11... | collective-permute-start | bytes 786440 | tf_op jit(solution)/shard_map/ppermute | solution.py:15
  10.6 16.1 %collective-permute-start.5 = (bf16[2,256,256]{2,1,0:T(8,128)(2,1)S(1)}, bf16[2,256,256]{2,1,0:T(8,128)(2,1)}, u32[]{:S(2)}, u32[]{:S(2)}) collective-permute-start(bf16[2,256,256]{2,1,0:T(8,128)(2,1)S(1)} %dynamic-slice_convert_fusion.after_ref), channel_id=1, source_target_pairs={{0,2},{1,3},{2,0},{3,1},{4,6},{5,7},{6,4},{7,5},{8,10},{9,11},{10,... | collective-permute-start | bytes 786440 | tf_op jit(solution)/shard_map/ppermute | solution.py:15
  13.7 8.4 %collective-permute-start.1 = (f32[2,256]{1,0:T(2,128)S(1)}, f32[2,256]{1,0:T(2,128)S(1)}, u32[]{:S(2)}, u32[]{:S(2)}) collective-permute-start(f32[2,256]{1,0:T(2,128)S(1)} %add.64), channel_id=1, source_target_pairs={{0,2},{1,3},{2,0},{3,1},{4,6},{5,7},{6,4},{7,5},{8,10},{9,11},{10,... | collective-permute-start | bytes 6152 | tf_op jit(solution)/shard_map/ppermute | solution.py:15
  14.4 3.4 %copy-start.1 = (bf16[1024,2,2048]{2,1,0:T(2,128)(2,1)S(1)}, bf16[1024,2,2048]{2,1,0:T(2,128)(2,1)}, u32[]{:S(2)}) copy-start(bf16[1024,2,2048]{2,1,0:T(2,128)(2,1)} %stored_ref.3) | copy-start | bytes 25165828
  19.9 1.9 %copy-start.3 = (bf16[2,512,2048]{2,1,0:T(8,128)(2,1)}, bf16[2,512,2048]{2,1,0:T(8,128)(2,1)S(1)}, u32[]{:S(2)}) copy-start(bf16[2,512,2048]{2,1,0:T(8,128)(2,1)S(1)} %shard_map.55) | copy-start | bytes 12582916
  25.3 14.0 %collective-permute-start.3 = (bf16[2,256,256]{1,2,0:T(8,128)(2,1)S(1)}, bf16[2,256,256]{1,2,0:T(8,128)(2,1)S(1)}, u32[]{:S(2)}, u32[]{:S(2)}) collective-permute-start(bf16[2,256,256]{1,2,0:T(8,128)(2,1)S(1)} %fusion.17), channel_id=1, source_target_pairs={{0,2},{1,3},{2,0},{3,1},{4,6},{5,7},{6,4},{7,5},{8,10},{9,11},{10,... | collective-permute-start | bytes 786440 | tf_op jit(solution)/shard_map/ppermute | solution.py:15
  27.8 18.2 %collective-permute-start.6 = (bf16[2,256,256]{2,1,0:T(8,128)(2,1)S(1)}, bf16[2,256,256]{2,1,0:T(8,128)(2,1)S(1)}, u32[]{:S(2)}, u32[]{:S(2)}) collective-permute-start(bf16[2,256,256]{2,1,0:T(8,128)(2,1)S(1)} %fusion.18.after_ref), channel_id=1, source_target_pairs={{0,1},{1,0},{2,3},{3,2},{4,5},{5,4},{6,7},{7,6},{8,9},{9,8},{10,11... | collective-permute-start | bytes 786440 | tf_op jit(solution)/shard_map/ppermute | solution.py:15
  40.4 9.4 %collective-permute-start.4 = (bf16[2,256,256]{1,2,0:T(8,128)(2,1)S(1)}, bf16[2,256,256]{1,2,0:T(8,128)(2,1)S(1)}, u32[]{:S(2)}, u32[]{:S(2)}) collective-permute-start(bf16[2,256,256]{1,2,0:T(8,128)(2,1)S(1)} %tanh_convert_fusion.1), channel_id=1, source_target_pairs={{0,1},{1,0},{2,3},{3,2},{4,5},{5,4},{6,7},{7,6},{8,9},{9,8},{10,11... | collective-permute-start | bytes 786440 | tf_op jit(solution)/shard_map/ppermute | solution.py:15
  40.5 3.4 %copy-start.2 = (bf16[1024,2,2048]{2,1,0:T(2,128)(2,1)S(1)}, bf16[1024,2,2048]{2,1,0:T(2,128)(2,1)}, u32[]{:S(2)}) copy-start(bf16[1024,2,2048]{2,1,0:T(2,128)(2,1)} %stored_ref.3) | copy-start | bytes 25165828
  43.9 5.9 %copy-start.4 = (bf16[2,512,2048]{2,1,0:T(8,128)(2,1)S(1)}, bf16[2,512,2048]{2,1,0:T(8,128)(2,1)}, u32[]{:S(2)}) copy-start(bf16[2,512,2048]{2,1,0:T(8,128)(2,1)} %copy-done.3) | copy-start | bytes 12582916
  47.1 14.2 %collective-permute-start.7 = (bf16[2,256,256]{2,1,0:T(8,128)(2,1)S(1)}, bf16[2,256,256]{2,1,0:T(8,128)(2,1)S(1)}, u32[]{:S(2)}, u32[]{:S(2)}) collective-permute-start(bf16[2,256,256]{2,1,0:T(8,128)(2,1)S(1)} %tanh_convert_fusion), channel_id=1, source_target_pairs={{0,2},{1,3},{2,0},{3,1},{4,6},{5,7},{6,4},{7,5},{8,10},{9,11},{10,... | collective-permute-start | bytes 786440 | tf_op jit(solution)/shard_map/ppermute | solution.py:15
